TPU v7x, 32 devices: a whole 2x2x4 slice. The times are simulated.
32 devices in a mesh: dp: 16 (over z, x, core), tensor: 2 (over y).
Axes of the slice: x: 2, y: 2, z: 4, core: 2. Of those that a mesh axis runs over, the one named last changes fastest.
Arguments:
- tokens: bfloat16 [32768, 512], P(('dp', 'tensor')), may hold values from -6 to 6
- cotangent: bfloat16 [32768, 512], P(('dp', 'tensor')), may hold values from -6 to 6
- w_qkv: bfloat16 [512, 3, 512], P(None, None, 'tensor'), may hold values from -0.25 to 0.25
- w_out: bfloat16 [512, 512], P('tensor'), may hold values from -1.5 to 1.5
- w_up: bfloat16 [512, 2048], P(None, 'tensor'), may hold values from -0.25 to 0.25
- w_down: bfloat16 [2048, 512], P('tensor'), may hold values from -0.125 to 0.125
- gains: float32 [2, 512], replicated, may hold values from 0.25 to 1.75
- shifts: float32 [2, 512], replicated, may hold values from -3 to 3
- feat_fresh: bfloat16 [64, 256], replicated, may hold values from -5 to 5
- feat_last: bfloat16 [64, 256], replicated, may hold values from -5 to 5
- flags: int32 [8], replicated, may hold values from 0 to 1, as said below
Outputs:
- block_out: float32 [32768, 512], P(('dp', 'tensor'))
- grad_tokens: float32 [32768, 512], P(('dp', 'tensor'))
- grad_qkv: float32 [512, 3, 512], P('dp', None, 'tensor')
- grad_wout: float32 [512, 512], P('tensor', 'dp')
- grad_up: float32 [512, 2048], P('dp', 'tensor')
- grad_down: float32 [2048, 512], P('tensor', 'dp')
- grad_gains: float32 [2, 512], replicated
- grad_shifts: float32 [2, 512], replicated
Inputs may be any that keep to these rules, and one draw needn't show every extreme that they name: `flags`: exactly half of the 8 heads take the fresh matrix.
All inputs are finite; a program needn't handle non-finite values.
Results may differ from a plain program's by a relative error of at most 0.029.
Values may be sent and summed in bfloat16 or wider, within the bound.
A program may use at most 192 MiB of HBM per device.

v0:
```python
import jax
import jax.numpy as jnp
from jax import lax
from jax.sharding import PartitionSpec as P

HEAD_DIM = 64
FEATURES = 256
BLOCK = 1024


EPS = 1e-05
HIGH = lax.Precision.HIGHEST


def normalize(inputs, norm_gain, offset):
    average = jnp.mean(inputs, axis=-1, keepdims=True)
    centered = inputs - average
    variance = jnp.mean(centered * centered, axis=-1, keepdims=True)
    return centered * lax.rsqrt(variance + EPS) * norm_gain + offset


def gelu_exact(inputs):
    return jax.nn.gelu(inputs, approximate=False)


def causal_table():
    row_index = lax.broadcasted_iota(jnp.int32, (BLOCK, BLOCK), 0)
    col_index = lax.broadcasted_iota(jnp.int32, (BLOCK, BLOCK), 1)
    return col_index <= row_index


def pick_features(flags, feat_fresh, feat_last, first_head, head_count):
    chosen = lax.dynamic_slice_in_dim(flags, first_head, head_count, 0)
    return jnp.where((chosen == 1)[:, None, None], feat_fresh[None], feat_last[None])


def split_heads(mixed_qkv, head_count):
    length = mixed_qkv.shape[0]
    shaped = mixed_qkv.reshape(length, 3, head_count, HEAD_DIM)
    return tuple((jnp.transpose(shaped[:, member], (1, 0, 2)) for member in range(3)))


def heads_of(matrix, head_count):
    length = matrix.shape[0]
    return jnp.transpose(matrix.reshape(length, head_count, HEAD_DIM), (1, 0, 2))


def join_heads(stacked):
    moved = jnp.transpose(stacked, (1, 0, 2))
    return moved.reshape(moved.shape[0], moved.shape[1] * moved.shape[2])


def to_blocks(stacked):
    shaped = stacked.reshape(
        (stacked.shape[0], stacked.shape[1] // BLOCK, BLOCK) + stacked.shape[2:]
    )
    return jnp.moveaxis(shaped, 1, 0)


def from_blocks(stacked):
    moved = jnp.moveaxis(stacked, 0, 1)
    return moved.reshape((moved.shape[0], moved.shape[1] * moved.shape[2]) + moved.shape[3:])


def features(inputs, projector):
    factor = HEAD_DIM ** (-0.25)
    projected = jnp.einsum("hlc,hcm->hlm", inputs, projector, preferred_element_type=jnp.float32)
    wide_in = inputs.astype(jnp.float32)
    squares = 0.5 * factor * factor * jnp.sum(wide_in * wide_in, axis=-1, keepdims=True)
    return jnp.exp(factor * projected - squares) * FEATURES ** (-0.5)


def features_back(inputs, projector, expo, grad_phi):
    factor = HEAD_DIM ** (-0.25)
    grad_pre = grad_phi * expo
    grad_proj = (factor * grad_pre).astype(jnp.bfloat16)
    wide_in = inputs.astype(jnp.float32)
    through = jnp.einsum("hlm,hcm->hlc", grad_proj, projector, preferred_element_type=jnp.float32)
    return through - factor * factor * jnp.sum(grad_pre, axis=-1, keepdims=True) * wide_in


def attend(phi_q, phi_k, values, memory_start, keys_start):
    causal = causal_table()

    def step(running, pieces):
        memory, key_sum = running
        block_q, block_k, block_v = pieces
        products = jnp.einsum("hcm,hkm->hck", block_q, block_k, preferred_element_type=jnp.float32)
        scores = jnp.where(causal, products, 0.0).astype(jnp.bfloat16)
        numerator = jnp.einsum("hck,hke->hce", scores, block_v, preferred_element_type=jnp.float32)
        numerator = numerator + jnp.einsum(
            "hcm,hme->hce", block_q, memory.astype(jnp.bfloat16), preferred_element_type=jnp.float32
        )
        denominator = jnp.sum(scores, axis=-1, dtype=jnp.float32)
        denominator = denominator + jnp.einsum(
            "hcm,hm->hc", block_q, key_sum.astype(jnp.bfloat16), preferred_element_type=jnp.float32
        )
        memory_next = memory + jnp.einsum(
            "hkm,hke->hme", block_k, block_v, preferred_element_type=jnp.float32
        )
        keys_next = key_sum + jnp.sum(block_k, axis=1, dtype=jnp.float32)
        return (
            (memory_next, keys_next),
            (numerator / denominator[..., None], denominator, memory, key_sum),
        )

    _, (outputs, denoms, memories, key_sums) = lax.scan(
        step, (memory_start, keys_start), (to_blocks(phi_q), to_blocks(phi_k), to_blocks(values))
    )
    return (from_blocks(outputs), from_blocks(denoms), memories, key_sums)


def attend_back(phi_q, phi_k, values, memories, key_sums, grad_num, grad_den, running_start):
    causal = causal_table()

    def step(running, pieces):
        grad_memory, grad_keys = running
        block_q, block_k, block_v, memory, key_sum, block_gn, block_gd = pieces
        products = jnp.einsum("hcm,hkm->hck", block_q, block_k, preferred_element_type=jnp.float32)
        scores = jnp.where(causal, products, 0.0).astype(jnp.bfloat16)
        grad_scores = (
            jnp.einsum("hce,hke->hck", block_gn, block_v, preferred_element_type=jnp.float32)
            + block_gd[..., None]
        )
        grad_prod = jnp.where(causal, grad_scores.astype(jnp.bfloat16), jnp.zeros((), jnp.bfloat16))
        round_memory = grad_memory.astype(jnp.bfloat16)
        key_low = key_sum.astype(jnp.bfloat16).astype(jnp.float32)
        grad_q = jnp.einsum("hck,hkm->hcm", grad_prod, block_k, preferred_element_type=jnp.float32)
        grad_q = grad_q + jnp.einsum(
            "hce,hme->hcm",
            block_gn,
            memory.astype(jnp.bfloat16),
            preferred_element_type=jnp.float32,
        )
        grad_q = grad_q + block_gd[..., None] * key_low[:, None, :]
        grad_k = jnp.einsum("hck,hcm->hkm", grad_prod, block_q, preferred_element_type=jnp.float32)
        grad_k = grad_k + jnp.einsum(
            "hke,hme->hkm", block_v, round_memory, preferred_element_type=jnp.float32
        )
        grad_k = grad_k + grad_keys[:, None, :]
        grad_v = jnp.einsum("hck,hce->hke", scores, block_gn, preferred_element_type=jnp.float32)
        grad_v = grad_v + jnp.einsum(
            "hkm,hme->hke", block_k, round_memory, preferred_element_type=jnp.float32
        )
        memory_next = grad_memory + jnp.einsum(
            "hcm,hce->hme", block_q, block_gn, preferred_element_type=jnp.float32
        )
        keys_next = grad_keys + jnp.einsum(
            "hcm,hc->hm", block_q.astype(jnp.float32), block_gd, precision=HIGH
        )
        return ((memory_next, keys_next), (grad_q, grad_k, grad_v))

    pieces = (
        to_blocks(phi_q),
        to_blocks(phi_k),
        to_blocks(values),
        memories,
        key_sums,
        to_blocks(grad_num),
        to_blocks(grad_den),
    )
    _, (grad_q, grad_k, grad_v) = lax.scan(step, running_start, pieces, reverse=True)
    return (from_blocks(grad_q), from_blocks(grad_k), from_blocks(grad_v))


def grads_start(outputs, denoms, grad_outputs):
    grad_num = (grad_outputs / denoms[..., None]).astype(jnp.bfloat16)
    grad_den = -jnp.sum(grad_outputs * outputs, axis=-1) / denoms
    return (grad_num, grad_den)


def grads_finish(
    queries,
    key_rows,
    values,
    projector,
    expo_q,
    expo_k,
    memories,
    key_sums,
    grad_num,
    grad_den,
    running_start,
):
    phi_q = expo_q.astype(jnp.bfloat16)
    phi_k = expo_k.astype(jnp.bfloat16)
    grad_phi_q, grad_phi_k, grad_values = attend_back(
        phi_q, phi_k, values, memories, key_sums, grad_num, grad_den, running_start
    )
    grad_queries = features_back(queries, projector, expo_q, grad_phi_q)
    grad_keys = features_back(key_rows, projector, expo_k, grad_phi_k)
    return jnp.stack(
        [join_heads(grad_queries), join_heads(grad_keys), join_heads(grad_values)], axis=1
    ).astype(jnp.bfloat16)


def local(
    tokens, cotangent, w_qkv, w_out, w_up, w_down, gains, shifts, feat_fresh, feat_last, flags
):
    inputs = tokens.astype(jnp.float32)
    normed, first_pull = jax.vjp(normalize, inputs, gains[0], shifts[0])
    normed_low = normed.astype(jnp.bfloat16)
    all_normed, all_cot = (
        lax.all_gather(normed_low, "tensor", axis=0, tiled=True),
        lax.all_gather(cotangent, "tensor", axis=0, tiled=True),
    )
    head_count = w_qkv.shape[2] // HEAD_DIM
    projector = pick_features(
        flags, feat_fresh, feat_last, lax.axis_index("tensor") * head_count, head_count
    )
    mixed_qkv = jnp.einsum(
        "ld,dce->lce", all_normed, w_qkv, preferred_element_type=jnp.float32
    ).astype(jnp.bfloat16)
    queries, key_rows, values = split_heads(mixed_qkv, head_count)
    expo_q = features(queries, projector)
    expo_k = features(key_rows, projector)
    zero_memory = jnp.zeros((head_count, FEATURES, HEAD_DIM), jnp.float32)
    zero_keys = jnp.zeros((head_count, FEATURES), jnp.float32)
    outputs, denoms, memories, key_sums = attend(
        expo_q.astype(jnp.bfloat16), expo_k.astype(jnp.bfloat16), values, zero_memory, zero_keys
    )
    joined = join_heads(outputs).astype(jnp.bfloat16)
    residual = inputs + lax.psum_scatter(
        jnp.dot(joined, w_out, preferred_element_type=jnp.float32),
        "tensor",
        scatter_dimension=0,
        tiled=True,
    )
    second_normed, second_pull = jax.vjp(normalize, residual, gains[1], shifts[1])
    all_second = lax.all_gather(second_normed.astype(jnp.bfloat16), "tensor", axis=0, tiled=True)
    pre_act = jnp.dot(all_second, w_up, preferred_element_type=jnp.float32)
    activated, gelu_pull = jax.vjp(gelu_exact, pre_act)
    act_low = activated.astype(jnp.bfloat16)
    result = residual + lax.psum_scatter(
        jnp.dot(act_low, w_down, preferred_element_type=jnp.float32).astype(jnp.bfloat16),
        "tensor",
        scatter_dimension=0,
        tiled=True,
    ).astype(jnp.float32)
    grad_act = jnp.einsum("ld,fd->lf", all_cot, w_down, preferred_element_type=jnp.float32)
    grad_pre = gelu_pull(grad_act)[0].astype(jnp.bfloat16)
    grad_down = jnp.einsum("lf,ld->fd", act_low, all_cot, preferred_element_type=jnp.float32)
    grad_up = jnp.einsum("ld,lf->df", all_second, grad_pre, preferred_element_type=jnp.float32)
    grad_second = lax.psum_scatter(
        jnp.einsum("lf,df->ld", grad_pre, w_up, preferred_element_type=jnp.float32),
        "tensor",
        scatter_dimension=0,
        tiled=True,
    )
    grad_resid, grad_gain2, grad_shift2 = second_pull(grad_second)
    grad_resid = grad_resid + cotangent.astype(jnp.float32)
    all_grad_resid = lax.all_gather(grad_resid.astype(jnp.bfloat16), "tensor", axis=0, tiled=True)
    grad_joined = jnp.einsum("ld,ed->le", all_grad_resid, w_out, preferred_element_type=jnp.float32)
    grad_wout = jnp.einsum("le,ld->ed", joined, all_grad_resid, preferred_element_type=jnp.float32)
    grad_num, grad_den = grads_start(outputs, denoms, heads_of(grad_joined, head_count))
    grad_mixed = grads_finish(
        queries,
        key_rows,
        values,
        projector,
        expo_q,
        expo_k,
        memories,
        key_sums,
        grad_num,
        grad_den,
        (zero_memory, zero_keys),
    )
    grad_wqkv = jnp.einsum(
        "ld,lce->dce", all_normed, grad_mixed, preferred_element_type=jnp.float32
    )
    grad_normed = lax.psum_scatter(
        jnp.einsum("lce,dce->ld", grad_mixed, w_qkv, preferred_element_type=jnp.float32),
        "tensor",
        scatter_dimension=0,
        tiled=True,
    )
    grad_wqkv, grad_wout, grad_up, grad_down = (
        lax.psum_scatter(grad_wqkv, "dp", scatter_dimension=0, tiled=True),
        lax.psum_scatter(grad_wout, "dp", scatter_dimension=1, tiled=True),
        lax.psum_scatter(grad_up, "dp", scatter_dimension=0, tiled=True),
        lax.psum_scatter(grad_down, "dp", scatter_dimension=1, tiled=True),
    )
    grad_inputs, grad_gain1, grad_shift1 = first_pull(grad_normed)
    grad_tokens = grad_resid + grad_inputs
    grad_gains, grad_shifts = lax.psum(
        (jnp.stack([grad_gain1, grad_gain2]), jnp.stack([grad_shift1, grad_shift2])),
        ("dp", "tensor"),
    )
    return (result, grad_tokens, grad_wqkv, grad_wout, grad_up, grad_down, grad_gains, grad_shifts)


def solution(mesh):
    placed = (
        P(("dp", "tensor"), None),
        P(("dp", "tensor"), None),
        P(None, None, "tensor"),
        P("tensor", None),
        P(None, "tensor"),
        P("tensor", None),
        P(),
        P(),
        P(),
        P(),
        P(),
    )
    return jax.shard_map(
        local,
        mesh=mesh,
        in_specs=placed,
        out_specs=(
            P(("dp", "tensor"), None),
            P(("dp", "tensor"), None),
            P("dp", None, "tensor"),
            P("tensor", "dp"),
            P("dp", "tensor"),
            P("tensor", "dp"),
            P(),
            P(),
        ),
        check_vma=False,
    )
```

profile of v0, /device:TPU:0, one launch (start us, length us, event | category | flops | bytes accessed | tf_op | source)
XLA Modules:
  0.0 849.4 jit_solution(16050850582295788397)
XLA Ops:
  15.6 35.8 %all-gather.5.cloned.1.call-done = bf16[2048,512]{1,0:T(8,128)(2,1)} async-done(((bf16[1024,512]{1,0:T(8,128)(2,1)}), bf16[2048,512]{1,0:T(8,128)(2,1)}) %all-gather.5.cloned.1.call-update) | async-done | bytes 2097168 | tf_op jit(solution)/shard_map/all_gather | solution.py:204
  69.5 39.9 %while.47 = (s32[]{:T(128)}, f32[4,256,64]{1,2,0:T(8,128)S(1)}, f32[4,256]{1,0:T(4,128)S(1)}, f32[2,4,1024,64]{2,3,1,0:T(8,128)}, f32[2,4,1024]{2,1,0:T(4,128)S(...) while((s32[]{:T(128)}, f32[4,256,64]{1,2,0:T(8,128)S(1)}, ...), condition=%wide.region_7.8_spmd.clone.clone, body=%wide.region_4.7_spmd.clone.sunk.clone | while | flops 2975599616 | bytes 87312640 | solution.py:107
  74.2 6.7 convert_reduce_fusion.8
  94.1 6.7 convert_reduce_fusion.8
  116.0 54.2 %reduce-scatter.9.cloned.1.call-done = f32[1024,512]{1,0:T(8,128)} async-done(((f32[2048,512]{1,0:T(8,128)}), f32[1024,512]{1,0:T(8,128)}) %reduce-scatter.9.cloned.1.call-update) | async-done | bytes 2097168 | tf_op jit(solution)/shard_map/reduce_scatter | solution.py:223
  175.5 32.6 %all-gather.7.cloned.1.call-done = bf16[2048,512]{1,0:T(8,128)(2,1)} async-done(((bf16[1024,512]{1,0:T(8,128)(2,1)}), bf16[2048,512]{1,0:T(8,128)(2,1)}) %all-gather.7.cloned.1.call-update) | async-done | bytes 2097168 | tf_op jit(solution)/shard_map/all_gather | solution.py:230
  208.1 23.0 %multiply_convert_fusion.2 = (bf16[2048,1024]{1,0:T(8,128)(2,1)}, f32[2048,1024]{1,0:T(8,128)}, f32[2048,1024]{1,0:T(8,128)}) fusion(bf16[2048,512]{1,0:T(8,128)(2,1)} %all-gather.7.cloned.1.call-done, bf16[512,1024]{1,0:T(8,128)(2,1)S(1)} %copy-done), kind=kOutput, calls=%fused_computation.122 | convolution fusion | flops 2283798528 | bytes 24117248 | tf_op jit(solution)/shard_map/dot_general | solution.py:231
  231.1 11.6 %all-gather.9.cloned.1.call-done = bf16[2048,512]{1,0:T(8,128)(2,1)} async-done(((bf16[1024,512]{1,0:T(8,128)(2,1)}), bf16[2048,512]{1,0:T(8,128)(2,1)}) %all-gather.9.cloned.1.call-update) | async-done | bytes 2097168 | tf_op jit(solution)/shard_map/all_gather | solution.py:205
  242.6 9.0 %add_convert_fusion.1 = bf16[2048,1024]{1,0:T(8,128)(2,1)S(1)} fusion(f32[2048,1024]{1,0:T(8,128)} %get-tuple-element.546, f32[2048,1024]{1,0:T(8,128)} %get-tuple-element.562, bf16[2048,512]{1,0:T(8,128)(2,1)} %all-gather.9.cloned.1.call-done, bf16[1024,512]{1,0:T(8,128)(2,1)S(1)} %copy-done.49), kind=kOutput, calls=%fused_computation.121 | convolution fusion | flops 2176843776 | bytes 24117248 | tf_op jit(solution)/shard_map/ld,fd->lf/dot_general | solution.py:240
  258.0 5.8 convolution_convert_fusion.1
  264.0 48.6 %reduce-scatter.13.cloned.1.call-done = f32[1024,512]{1,0:T(8,128)} async-done(((f32[2048,512]{1,0:T(8,128)}), f32[1024,512]{1,0:T(8,128)}) %reduce-scatter.13.cloned.1.call-update) | async-done | bytes 2097168 | tf_op jit(solution)/shard_map/reduce_scatter | solution.py:244
  316.2 31.0 %reduce-scatter.11.cloned.1.call-done = bf16[1024,512]{1,0:T(8,128)(2,1)} async-done(((bf16[2048,512]{1,0:T(8,128)(2,1)}), bf16[1024,512]{1,0:T(8,128)(2,1)}) %reduce-scatter.11.cloned.1.call-update) | async-done | bytes 1048592 | tf_op jit(solution)/shard_map/reduce_scatter | solution.py:234
  354.9 32.1 %all-gather.11.cloned.1.call-done = bf16[2048,512]{1,0:T(8,128)(2,1)} async-done(((bf16[1024,512]{1,0:T(8,128)(2,1)}), bf16[2048,512]{1,0:T(8,128)(2,1)}) %all-gather.11.cloned.1.call-update) | async-done | bytes 2097168 | tf_op jit(solution)/shard_map/all_gather | solution.py:252
  399.2 90.1 %while.48 = (s32[]{:T(128)}, f32[4,256,64]{1,2,0:T(8,128)S(1)}, f32[4,256]{1,0:T(4,128)S(1)}, f32[2,4,1024,256]{3,2,1,0:T(8,128)}, f32[2,4,1024,256]{3,2,1,0:T(8...) while((s32[]{:T(128)}, f32[4,256,64]{1,2,0:T(8,128)S(1)}, ...), condition=%wide.region_17.18_spmd.clone.clone.clone, body=%wide.region_16.17_spmd.clone.clone.sunk.clone | while | flops 8097631232 | bytes 111422200 | solution.py:162
  411.4 7.4 fusion.314
  426.8 8.5 fusion.313
  435.3 6.3 fusion.311
  451.6 7.4 fusion.314
  467.1 8.5 fusion.313
  475.6 6.3 fusion.311
  489.3 7.7 copy.38
  503.5 14.3 %fusion.181 = (f32[4,2048]{1,0:T(4,128)S(1)}, f32[4,2048,256]{2,1,0:T(8,128)S(1)}, f32[4,2048]{1,0:T(4,128)S(1)}, f32[4,2048,256]{2,1,0:T(8,128)}) fusion(f32[4,2048]{1,0:T(4,128)S(1)} %copy-done.31, f32[4,2048,256]{2,1,0:T(8,128)} %get-tuple-element.561, f32[4,2,1024,256]{3,2,1,0:T(8,128)} %copy.38, f32[4,2048]{1,0:T(4,128)S(1)} %copy-done.33, ...), kind=kLoop, calls=%fused_computation.236 | loop fusion | flops 20955136 | bytes 50462720 | tf_op jit(solution)/shard_map/reduce_sum | solution.py:79
  528.4 5.6 convolution_bitcast_fusion
  535.6 5.9 fusion.191
  541.6 6.7 fusion.192
  550.5 5.6 fusion.146
  556.2 32.5 %reduce-scatter.15.cloned.1.call-done = f32[1024,512]{1,0:T(8,128)} async-done(((f32[2048,512]{1,0:T(8,128)}), f32[1024,512]{1,0:T(8,128)}) %reduce-scatter.15.cloned.1.call-update) | async-done | bytes 2097168 | tf_op jit(solution)/shard_map/reduce_scatter | solution.py:272
  592.4 39.7 %all-reduce = (f32[2,512]{1,0:T(2,128)}, f32[2,512]{1,0:T(2,128)}) all-reduce(f32[2,512]{1,0:T(2,128)S(1)} %pad_maximum_fusion.3, f32[2,512]{1,0:T(2,128)S(1)} %pad_maximum_fusion.4), channel_id=1, replica_groups=mesh['dp'=16,'tensor'=2] {'dp','tensor'}, use_global_device_ids=true, to_apply=%region_29.30 | all-reduce | flops 2048 | bytes 16384 | tf_op jit(solution)/shard_map/psum | solution.py:286
  635.9 19.3 %reduce-scatter.21.cloned.1.call-done = f32[32,1024]{1,0:T(8,128)} async-done(((f32[512,1024]{1,0:T(8,128)}), f32[32,1024]{1,0:T(8,128)}) %reduce-scatter.21.cloned.1.call-update) | async-done | bytes 131088 | tf_op jit(solution)/shard_map/reduce_scatter | solution.py:281
  655.2 64.9 %reduce-scatter.23.cloned.1.call-done = f32[1024,32]{0,1:T(8,128)} async-done(((f32[1024,512]{0,1:T(8,128)}), f32[1024,32]{0,1:T(8,128)}) %reduce-scatter.23.cloned.1.call-update) | async-done | bytes 131088 | tf_op jit(solution)/shard_map/reduce_scatter | solution.py:282
  720.1 59.3 %reduce-scatter.19.cloned.1.call-done = f32[256,32]{0,1:T(8,128)} async-done(((f32[256,512]{0,1:T(8,128)}), f32[256,32]{0,1:T(8,128)}) %reduce-scatter.19.cloned.1.call-update) | async-done | bytes 32784 | tf_op jit(solution)/shard_map/reduce_scatter | solution.py:280
  779.4 62.7 %reduce-scatter.17.cloned.1.call-done = f32[32,3,256]{2,0,1:T(8,128)} async-done(((f32[512,3,256]{2,0,1:T(8,128)}), f32[32,3,256]{2,0,1:T(8,128)}) %reduce-scatter.17.cloned.1.call-update) | async-done | bytes 98320 | tf_op jit(solution)/shard_map/reduce_scatter | solution.py:279
  (262 shorter events, 158.7 us)
Async XLA Ops:
  7.2 200.9 %copy-start = (bf16[512,1024]{1,0:T(8,128)(2,1)S(1)}, bf16[512,1024]{1,0:T(8,128)(2,1)}, u32[]{:S(2)}) copy-start(bf16[512,1024]{1,0:T(8,128)(2,1)} %param.19) | copy-start | bytes 3145732
  7.2 8.3 copy-start.51
  7.2 44.1 %copy-start.50 = (bf16[512,3,256]{2,0,1:T(8,128)(2,1)S(1)}, bf16[512,3,256]{2,0,1:T(8,128)(2,1)}, u32[]{:S(2)}) copy-start(bf16[512,3,256]{2,0,1:T(8,128)(2,1)} %param.17) | copy-start | bytes 2359300
  7.2 44.1 %all-gather.5.cloned.1.call-start = ((), (), s32[]{:S(2)}) async-start(), calls=%async_computation.8 | async-start | bytes 3145728 | tf_op jit(solution)/shard_map/all_gather | solution.py:204
  15.3 154.9 %reduce-scatter.9.cloned.1.call-start = ((), (), s32[]{:S(2)}) async-start(), calls=%async_computation.9 | async-start | bytes 6291456 | tf_op jit(solution)/shard_map/reduce_scatter | solution.py:223
  15.6 47.1 %copy-start.46 = (pred[4]{0:T(512)(128)(4,1)}, pred[4]{0:T(512)(128)(4,1)S(1)}, u32[]{:S(2)}) copy-start(pred[4]{0:T(512)(128)(4,1)S(1)} %dynamic-slice_compare_fusion) | copy-start | bytes 16
  115.7 54.6 %copy-start.7 = (bf16[1024,512]{1,0:T(8,128)(2,1)S(1)}, bf16[1024,512]{1,0:T(8,128)(2,1)}, u32[]{:S(2)}) copy-start(bf16[1024,512]{1,0:T(8,128)(2,1)} %param.15) | copy-start | bytes 3145732
  115.7 92.4 %all-gather.7.cloned.1.call-start = ((), (), s32[]{:S(2)}) async-start(), calls=%async_computation.10 | async-start | bytes 3145728 | tf_op jit(solution)/shard_map/all_gather | solution.py:230
  174.8 67.8 %all-gather.9.cloned.1.call-start = ((), (), s32[]{:S(2)}) async-start(), calls=%async_computation.12 | async-start | bytes 3145728 | tf_op jit(solution)/shard_map/all_gather | solution.py:205
  175.4 67.2 %copy-start.49 = (bf16[1024,512]{1,0:T(8,128)(2,1)S(1)}, bf16[1024,512]{1,0:T(8,128)(2,1)}, u32[]{:S(2)}) copy-start(bf16[1024,512]{1,0:T(8,128)(2,1)} %param.20) | copy-start | bytes 3145732
  175.4 137.1 %reduce-scatter.13.cloned.1.call-start = ((), (), s32[]{:S(2)}) async-start(), calls=%async_computation.13 | async-start | bytes 6291456 | tf_op jit(solution)/shard_map/reduce_scatter | solution.py:244
  258.0 89.1 %reduce-scatter.11.cloned.1.call-start = ((), (), s32[]{:S(2)}) async-start(), calls=%async_computation.11 | async-start | bytes 3145728 | tf_op jit(solution)/shard_map/reduce_scatter | solution.py:234
  263.9 123.0 %all-gather.11.cloned.1.call-start = ((), (), s32[]{:S(2)}) async-start(), calls=%async_computation.14 | async-start | bytes 3145728 | tf_op jit(solution)/shard_map/all_gather | solution.py:252
  316.2 36.2 %copy-start.13 = (bf16[1024,512]{1,0:T(8,128)(2,1)S(1)}, bf16[1024,512]{1,0:T(8,128)(2,1)}, u32[]{:S(2)}) copy-start(bf16[1024,512]{1,0:T(8,128)(2,1)} %param.16) | copy-start | bytes 3145732
  353.7 234.9 %reduce-scatter.15.cloned.1.call-start = ((), (), s32[]{:S(2)}) async-start(), calls=%async_computation.15 | async-start | bytes 6291456 | tf_op jit(solution)/shard_map/reduce_scatter | solution.py:272
  503.5 14.3 %copy-start.27 = (bf16[64,256]{1,0:T(8,128)(2,1)S(1)}, bf16[64,256]{1,0:T(8,128)(2,1)}, u32[]{:S(2)}) copy-start(bf16[64,256]{1,0:T(8,128)(2,1)} %param.24) | copy-start | bytes 98308
  503.5 14.3 %copy-start.29 = (bf16[64,256]{1,0:T(8,128)(2,1)S(1)}, bf16[64,256]{1,0:T(8,128)(2,1)}, u32[]{:S(2)}) copy-start(bf16[64,256]{1,0:T(8,128)(2,1)} %param.23) | copy-start | bytes 98308
  503.5 14.3 %copy-start.47 = (pred[4]{0:T(512)(128)(4,1)S(1)}, pred[4]{0:T(512)(128)(4,1)}, u32[]{:S(2)}) copy-start(pred[4]{0:T(512)(128)(4,1)} %copy-done.46) | copy-start | bytes 16
  534.1 121.1 %reduce-scatter.21.cloned.1.call-start = ((), (), s32[]{:S(2)}) async-start(), calls=%async_computation.18 | async-start | bytes 2228224 | tf_op jit(solution)/shard_map/reduce_scatter | solution.py:281
  541.6 178.5 %reduce-scatter.23.cloned.1.call-start = ((), (), s32[]{:S(2)}) async-start(), calls=%async_computation.19 | async-start | bytes 2228224 | tf_op jit(solution)/shard_map/reduce_scatter | solution.py:282
  548.4 231.0 %reduce-scatter.19.cloned.1.call-start = ((), (), s32[]{:S(2)}) async-start(), calls=%async_computation.17 | async-start | bytes 557056 | tf_op jit(solution)/shard_map/reduce_scatter | solution.py:280
  550.4 38.2 %copy-start.8 = (bf16[1024,512]{1,0:T(8,128)(2,1)S(1)}, bf16[1024,512]{1,0:T(8,128)(2,1)}, u32[]{:S(2)}) copy-start(bf16[1024,512]{1,0:T(8,128)(2,1)} %param.15) | copy-start | bytes 3145732
  550.4 38.2 %copy-start.35 = (f32[1024]{0:T(1024)S(1)}, f32[1024]{0:T(1024)}, u32[]{:S(2)}) copy-start(f32[1024]{0:T(1024)} %copy-done.34) | copy-start | bytes 12292
  550.5 38.2 %copy-start.39 = (f32[1,512]{1,0:T(1,128)S(1)}, f32[1,512]{1,0:T(1,128)}, u32[]{:S(2)}) copy-start(f32[1,512]{1,0:T(1,128)} %copy-done.38) | copy-start | bytes 6148
  550.5 291.6 %reduce-scatter.17.cloned.1.call-start = ((), (), s32[]{:S(2)}) async-start(), calls=%async_computation.16 | async-start | bytes 1671168 | tf_op jit(solution)/shard_map/reduce_scatter | solution.py:279
  556.1 34.9 %copy-start.45 = (f32[512]{0:T(512)S(1)}, f32[512]{0:T(512)}, u32[]{:S(2)}) copy-start(f32[512]{0:T(512)} %get-tuple-element.486) | copy-start | bytes 6148
  556.1 35.0 %copy-start.43 = (f32[1024]{0:T(1024)S(1)}, f32[1024]{0:T(1024)}, u32[]{:S(2)}) copy-start(f32[1024]{0:T(1024)} %copy-done.42) | copy-start | bytes 12292
  556.1 35.0 %copy-start.37 = (f32[1024]{0:T(1024)S(1)}, f32[1024]{0:T(1024)}, u32[]{:S(2)}) copy-start(f32[1024]{0:T(1024)} %copy-done.36) | copy-start | bytes 12292
  556.1 36.2 %copy-start.44 = (f32[512]{0:T(512)S(1)}, f32[512]{0:T(512)}, u32[]{:S(2)}) copy-start(f32[512]{0:T(512)} %get-tuple-element.478) | copy-start | bytes 6148
  556.1 76.0 %copy-start.14 = (bf16[1024,512]{1,0:T(8,128)(2,1)S(1)}, bf16[1024,512]{1,0:T(8,128)(2,1)}, u32[]{:S(2)}) copy-start(bf16[1024,512]{1,0:T(8,128)(2,1)} %param.16) | copy-start | bytes 3145732
  556.1 76.0 %copy-start.41 = (f32[1024]{0:T(1024)S(1)}, f32[1024]{0:T(1024)}, u32[]{:S(2)}) copy-start(f32[1024]{0:T(1024)} %copy-done.40) | copy-start | bytes 12292
  632.1 210.0 %copy-start.1 = (bf16[512,1024]{1,0:T(8,128)(2,1)S(1)}, bf16[512,1024]{1,0:T(8,128)(2,1)}, u32[]{:S(2)}) copy-start(bf16[512,1024]{1,0:T(8,128)(2,1)} %param.19) | copy-start | bytes 3145732
  (44 other events, 179.3 us)
Sparse Core Ops, SparseCore 0:
  15.5 35.8 all-gather.4
  115.9 54.3 reduce-scatter.8
  175.0 33.0 all-gather.6
  209.5 33.0 all-gather.8
  258.1 54.3 reduce-scatter.12
  315.2 31.8 reduce-scatter.10
  353.8 33.0 all-gather.10
  534.2 54.3 reduce-scatter.14
  592.9 62.1 reduce-scatter.20
  659.3 60.7 reduce-scatter.22
  724.2 55.1 reduce-scatter.18
  783.5 58.5 reduce-scatter.16
where the time goes:
time: 859 us; the launch traced here: 849 us
  waiting for transfers between devices  485 us (56%)
  matrix products  203 us (24%)
  local copies, waits for them, and re-layouts  48.1 us (6%)
  other arithmetic  47.7 us (6%)
  blocking collectives  39.7 us (5%)
  between operations  15.4 us (2%)
  loops' own time  9.78 us (1%)
    reduce_scatter x1, waiting for transfers between devices, local(): lax.psum_scatter(grad_down, 'dp', scatter_dimension=1, tiled=True)  64.9 us
    reduce_scatter x1, waiting for transfers between devices, local(): lax.psum_scatter(grad_wqkv, 'dp', scatter_dimension=0, tiled=True)  62.7 us
    reduce_scatter x1, waiting for transfers between devices, local(): lax.psum_scatter(grad_wout, 'dp', scatter_dimension=1, tiled=True)  59.3 us
    reduce_scatter x1, waiting for transfers between devices, local(): lax.psum_scatter(jnp.dot(joined, w_out, preferred_element_type=jnp.float3...  54.2 us
    reduce_scatter x1, waiting for transfers between devices, local(): lax.psum_scatter(jnp.einsum('lf,df->ld', grad_pre, w_up, preferred_elemen...  48.6 us
    psum x1, blocking collectives, local(): lax.psum((jnp.stack([grad_gain1, grad_gain2]), jnp.stack([grad_shift1, gr...  39.7 us
    all_gather x1, waiting for transfers between devices, local(): lax.all_gather(normed_low, 'tensor', axis=0, tiled=True)  35.8 us
    all_gather x1, waiting for transfers between devices, local(): lax.all_gather(second_normed.astype(jnp.bfloat16), 'tensor', axis=0, tile...  32.6 us
  transfers between devices with their start and end apart: 12, of which 12 were waited for; matrix products, arithmetic and copies ran while one was open for 7% of the time, Pallas kernels for 0%

commit v1 on v0

v1 whole, which is shorter than its diff:
```python
import jax
import jax.numpy as jnp
from jax import lax
from jax.sharding import PartitionSpec as P

HEAD_DIM = 64
FEATURES = 256
EPS = 1e-05
F32 = jnp.float32
BF16 = jnp.bfloat16


def normalize(inputs, norm_gain, offset):
    average = jnp.mean(inputs, axis=-1, keepdims=True)
    centered = inputs - average
    variance = jnp.mean(centered * centered, axis=-1, keepdims=True)
    return centered * lax.rsqrt(variance + EPS) * norm_gain + offset


def gelu_exact(inputs):
    return jax.nn.gelu(inputs, approximate=False)


def mul(spec, *operands):
    return jnp.einsum(spec, *operands, preferred_element_type=F32)


def split_heads(matrix):
    length = matrix.shape[0]
    return jnp.transpose(matrix.reshape(length, -1, HEAD_DIM), (1, 0, 2))


def join_heads(stacked):
    moved = jnp.transpose(stacked, (1, 0, 2))
    return moved.reshape(moved.shape[0], -1)


def features(inputs, projector):
    factor = HEAD_DIM ** (-0.25)
    projected = mul("hlc,hcm->hlm", inputs, projector)
    wide_in = inputs.astype(F32)
    squares = 0.5 * factor * factor * jnp.sum(wide_in * wide_in, axis=-1, keepdims=True)
    return jnp.exp(factor * projected - squares) * FEATURES ** (-0.5)


def features_back(inputs, projector, expo, grad_phi):
    factor = HEAD_DIM ** (-0.25)
    grad_pre = grad_phi * expo
    grad_proj = (factor * grad_pre).astype(BF16)
    through = mul("hlm,hcm->hlc", grad_proj, projector)
    return through - factor * factor * jnp.sum(grad_pre, axis=-1, keepdims=True) * inputs.astype(F32)


def from_others(part, before):
    parts = lax.all_gather(part, "tensor")
    mine = lax.axis_index("tensor")
    place = jnp.arange(parts.shape[0])
    taken = (place < mine) if before else (place > mine)
    return jnp.sum(jnp.where(taken[:, None, None, None], parts, 0.0), axis=0)


def with_sums(values):
    return jnp.concatenate([values, jnp.ones_like(values[..., :1])], axis=-1)


def plain(
    tokens, cotangent, w_qkv, w_out, w_up, w_down, gains, shifts, feat_fresh, feat_last, flags
):
    w_qkv = lax.all_gather(w_qkv, "tensor", axis=2, tiled=True)
    w_out = lax.all_gather(w_out, "tensor", axis=0, tiled=True)
    w_up = lax.all_gather(w_up, "tensor", axis=1, tiled=True)
    w_down = lax.all_gather(w_down, "tensor", axis=0, tiled=True)
    inputs = tokens.astype(F32)
    rows = inputs.shape[0]
    normed, first_pull = jax.vjp(normalize, inputs, gains[0], shifts[0])
    normed = normed.astype(BF16)
    projector = jnp.where((flags == 1)[:, None, None], feat_fresh[None], feat_last[None])
    mixed = mul("ld,dce->cle", normed, w_qkv).astype(BF16)
    queries, keys, values = (split_heads(mixed[c]) for c in range(3))
    expo_q, expo_k = features(queries, projector), features(keys, projector)
    phi_q, phi_k = expo_q.astype(BF16), expo_k.astype(BF16)
    summed_values = with_sums(values)
    memory = from_others(mul("hkm,hke->hme", phi_k, summed_values), True).astype(BF16)
    causal = jnp.tril(jnp.ones((rows, rows), jnp.bool_))
    scores = jnp.where(causal, mul("hcm,hkm->hck", phi_q, phi_k), 0.0).astype(BF16)
    both = mul("hck,hke->hce", scores, summed_values) + mul("hcm,hme->hce", phi_q, memory)
    denoms = both[..., -1:]
    outputs = both[..., :-1] / denoms
    joined = join_heads(outputs).astype(BF16)
    residual = inputs + mul("le,ed->ld", joined, w_out)
    second, second_pull = jax.vjp(normalize, residual, gains[1], shifts[1])
    second = second.astype(BF16)
    pre_act = mul("ld,df->lf", second, w_up)
    activated, gelu_pull = jax.vjp(gelu_exact, pre_act)
    act_low = activated.astype(BF16)
    result = residual + mul("lf,fd->ld", act_low, w_down)
    grad_act = mul("ld,fd->lf", cotangent, w_down)
    grad_pre = gelu_pull(grad_act)[0].astype(BF16)
    grad_down = mul("ld,lf->df", cotangent, act_low)
    grad_up = mul("ld,lf->df", second, grad_pre)
    grad_resid, grad_gain2, grad_shift2 = second_pull(mul("lf,df->ld", grad_pre, w_up))
    grad_resid = grad_resid + cotangent.astype(F32)
    resid_low = grad_resid.astype(BF16)
    grad_out = split_heads(mul("ld,ed->le", resid_low, w_out))
    grad_wout = mul("ld,le->de", resid_low, joined)
    grad_num = (grad_out / denoms).astype(BF16)
    grad_den = -jnp.sum(grad_out * outputs, axis=-1, keepdims=True) / denoms
    grad_both = jnp.concatenate([grad_num, grad_den.astype(BF16)], axis=-1)
    grad_memory = from_others(mul("hcm,hce->hme", phi_q, grad_both), False).astype(BF16)
    grad_scores = jnp.where(
        causal, (mul("hce,hke->hck", grad_num, values) + grad_den).astype(BF16), 0
    )
    grad_q = mul("hck,hkm->hcm", grad_scores, phi_k) + mul("hce,hme->hcm", grad_both, memory)
    grad_k = mul("hck,hcm->hkm", grad_scores, phi_q)
    grad_k = grad_k + mul("hke,hme->hkm", summed_values, grad_memory)
    grad_v = mul("hck,hce->hke", scores, grad_num)
    grad_v = grad_v + mul("hkm,hme->hke", phi_k, grad_memory[..., :-1])
    grad_mixed = jnp.stack(
        [
            join_heads(features_back(queries, projector, expo_q, grad_q)),
            join_heads(features_back(keys, projector, expo_k, grad_k)),
            join_heads(grad_v),
        ]
    ).astype(BF16)
    grad_wqkv = mul("ld,cle->dce", normed, grad_mixed)
    grad_normed = mul("cle,dce->ld", grad_mixed, w_qkv)
    grad_inputs, grad_gain1, grad_shift1 = first_pull(grad_normed)
    grad_tokens = grad_resid + grad_inputs

    tensor, dp = lax.axis_size("tensor"), lax.axis_size("dp")
    wide = grad_wqkv.shape[0]

    def by_owner(grad):
        shaped = grad.reshape(dp, wide // dp, -1, tensor, grad.shape[-1] // tensor)
        moved = jnp.transpose(shaped, (0, 3, 1, 2, 4))
        return moved.reshape(dp * tensor, wide // dp, -1).astype(BF16)

    packed = jnp.concatenate(
        [by_owner(g) for g in (grad_wqkv, grad_wout, grad_up, grad_down)], axis=2
    )
    owned = lax.psum_scatter(packed, ("dp", "tensor"), scatter_dimension=0, tiled=True)[0]
    owned = owned.astype(F32)
    edge = [3 * wide // tensor, 4 * wide // tensor, 4 * wide // tensor + w_up.shape[1] // tensor]
    own_qkv, own_wout, own_up, own_down = jnp.split(owned, edge, axis=1)
    grad_gains, grad_shifts = lax.psum(
        (jnp.stack([grad_gain1, grad_gain2]), jnp.stack([grad_shift1, grad_shift2])),
        ("dp", "tensor"),
    )
    return (
        result,
        grad_tokens,
        own_qkv.reshape(wide // dp, 3, wide // tensor),
        own_wout.T,
        own_up,
        own_down.T,
        grad_gains,
        grad_shifts,
    )


def solution(mesh):
    placed = (
        P(("dp", "tensor"), None),
        P(("dp", "tensor"), None),
        P(None, None, "tensor"),
        P("tensor", None),
        P(None, "tensor"),
        P("tensor", None),
        P(),
        P(),
        P(),
        P(),
        P(),
    )
    return jax.shard_map(
        plain,
        mesh=mesh,
        in_specs=placed,
        out_specs=(
            P(("dp", "tensor"), None),
            P(("dp", "tensor"), None),
            P("dp", None, "tensor"),
            P("tensor", "dp"),
            P("dp", "tensor"),
            P("tensor", "dp"),
            P(),
            P(),
        ),
        check_vma=False,
    )
```

time: 859 us -> 430 us (0.50)
  waiting for transfers between devices: 485 us -> 96.1 us
  other arithmetic: 47.7 us -> 18.9 us
  matrix products: 203 us -> 176 us
  local copies, waits for them, and re-layouts: 48.1 us -> 64.1 us
  blocking collectives: 39.7 us -> 52.8 us
  loops' own time: 9.78 us -> 0 us
    reduce_scatter x8 -> x1, waiting for transfers between devices: 372 us -> 50.9 us  [plain(): lax.psum_scatter(packed, ('dp', 'tensor'), scatter_dimension=0, tiled=True)]
    all_gather x4 -> x5, waiting for transfers between devices: 112 us -> 44 us  [the longest x1 27.8 us: plain(): w_qkv = lax.all_gather(w_qkv, 'tensor', axis=2, tiled=True)]
    convert_element_type x0 -> x8, local copies, waits for them, and re-layouts: none -> 33 us  [by_owner(): return moved.reshape(dp * tensor, wide // dp, -1).astype(BF16)]
    dot_general x44 -> x28, matrix products: 203 us -> 176 us  [mul(): return jnp.einsum(spec, *operands, preferred_element_type=F32)]
    reduce_sum x3, other arithmetic: 18.3 us -> 3.4 us  [the longest x2 2.79 us: from_others(): return jnp.sum(jnp.where(taken[:, None, None, None], parts, 0.0), axis=0)]
    all_gather x0 -> x1, blocking collectives: none -> 12 us  [plain(): w_out = lax.all_gather(w_out, 'tensor', axis=0, tiled=True)]
    transpose x2, local copies, waits for them, and re-layouts: 12.6 us -> 1.33 us  [plain(): return (result, grad_tokens, own_qkv.reshape(wide // dp, 3, wide // tenso...]
    another operation x2 -> x0, loops' own time: 9.78 us -> none  [the longest x1 9.65 us: attend_back(): lax.scan(step, running_start, pieces, reverse=True)]
  transfers between devices with their start and end apart: 12 -> 6, of which waited for: 12 -> 4; matrix products, arithmetic and copies ran while one was open for 7% -> 31% of each run, Pallas kernels for 0% -> 0%
where the time goes in v1:
time: 430 us; the launch traced here: 424 us
  matrix products  176 us (41%)
  waiting for transfers between devices  96.1 us (22%)
  local copies, waits for them, and re-layouts  64.1 us (15%)
  blocking collectives  52.8 us (12%)
  other arithmetic  18.9 us (4%)
  between operations  15.1 us (4%)
    dot_general x28, matrix products, mul(): return jnp.einsum(spec, *operands, preferred_element_type=F32)  176 us
    reduce_scatter x1, waiting for transfers between devices, plain(): lax.psum_scatter(packed, ('dp', 'tensor'), scatter_dimension=0, tiled=True)  50.9 us
    psum x1, blocking collectives, plain(): lax.psum((jnp.stack([grad_gain1, grad_gain2]), jnp.stack([grad_shift1, gr...  40.8 us
    convert_element_type x8, local copies, waits for them, and re-layouts, by_owner(): return moved.reshape(dp * tensor, wide // dp, -1).astype(BF16)  33 us
    all_gather x1, waiting for transfers between devices, plain(): w_qkv = lax.all_gather(w_qkv, 'tensor', axis=2, tiled=True)  27.8 us
    unnamed x115, local copies, waits for them, and re-layouts  17.7 us
    all_gather x1, blocking collectives, plain(): w_out = lax.all_gather(w_out, 'tensor', axis=0, tiled=True)  12 us
    all_gather x1, waiting for transfers between devices, plain(): w_down = lax.all_gather(w_down, 'tensor', axis=0, tiled=True)  10.4 us
  transfers between devices with their start and end apart: 6, of which 4 were waited for; matrix products, arithmetic and copies ran while one was open for 31% of the time, Pallas kernels for 0%

profile of v1, /device:TPU:0, one launch (start us, length us, event | category | flops | bytes accessed | tf_op | source)
XLA Modules:
  0.0 423.8 jit_solution(14544273571084177946)
XLA Ops:
  12.2 27.8 %all-gather.8.cloned.1.call-done = bf16[512,3,512]{0,2,1:T(8,128)(2,1)} async-done(((bf16[512,3,256]{0,2,1:T(8,128)(2,1)}), bf16[512,3,512]{0,2,1:T(8,128)(2,1)}) %all-gather.8.cloned.1.call-update) | async-done | bytes 1572880 | tf_op jit(solution)/shard_map/all_gather | solution.py:69
  44.3 4.5 %fusion.8 = (bf16[8,1024,256]{1,2,0:T(8,128)(2,1)S(1)}, f32[8,1024,256]{1,2,0:T(8,128)}) fusion(f32[8,1024]{1,0:T(8,128)S(1)} %broadcast_multiply_fusion, bf16[8,1024,64]{1,2,0:T(8,128)(2,1)S(1)} %bitcast.145, pred[8]{0:T(512)(128)(4,1)S(1)} %broadcast_compare_fusion, bf16[64,256]{1,0:T(8,128)(2,1)S(1)} %copy-done.29, bf16[64,256]{1,0:T(8,128)(2,1)S(1)} %copy-done.31), kind=kOutput, calls=%fused_computation.27 | convolution fusion | flops 276955136 | bytes 13729800 | tf_op jit(solution)/shard_map/hlc,hcm->hlm/dot_general | solution.py:25
  56.3 12.0 %all_gather.27 = bf16[512,512]{1,0:T(8,128)(2,1)} all-gather(bf16[256,512]{1,0:T(8,128)(2,1)S(1)} %copy-done.35), channel_id=1, replica_groups=mesh['dp'=16,'tensor'=2] {'tensor'}, dimensions={0}, use_global_device_ids=true | all-gather | bytes 786432 | tf_op jit(solution)/shard_map/all_gather | solution.py:70
  70.9 5.7 %fusion.7 = (bf16[8,1024,256]{1,2,0:T(8,128)(2,1)}, f32[8,1024,256]{1,2,0:T(8,128)}) fusion(f32[8,1024]{1,0:T(8,128)S(1)} %broadcast_multiply_fusion.1, bf16[8,1024,64]{1,2,0:T(8,128)(2,1)S(1)} %bitcast.148, pred[8]{0:T(512)(128)(4,1)S(1)} %broadcast_compare_fusion, bf16[64,256]{1,0:T(8,128)(2,1)S(1)} %copy-done.29, bf16[64,256]{1,0:T(8,128)(2,1)S(1)} %copy-done.31), kind=kOutput, calls=%fused_computation.26 | convolution fusion | flops 276955136 | bytes 13729800 | tf_op jit(solution)/shard_map/hlc,hcm->hlm/dot_general | solution.py:25
  76.6 11.8 %select_convert_fusion = bf16[8,1024,1024]{2,1,0:T(8,128)(2,1)} fusion(pred[1024,1024]{1,0:T(8,128)(4,1)S(1)} %copy-done.25, bf16[8,1024,256]{1,2,0:T(8,128)(2,1)} %get-tuple-element.72, bf16[8,1024,256]{1,2,0:T(8,128)(2,1)} %copy-done.3), kind=kOutput, calls=%fused_computation.1 | convolution fusion | flops 4311744512 | bytes 26214400 | tf_op jit(solution)/shard_map/hcm,hkm->hck/dot_general | solution.py:25
  88.4 10.0 %fusion.34 = f32[8,1024,65]{1,2,0:T(8,128)} fusion(bf16[8,1024,1024]{2,1,0:T(8,128)(2,1)} %select_convert_fusion, bf16[8,1024,64]{1,2,0:T(8,128)(2,1)S(1)} %bitcast.141), kind=kOutput, calls=%fused_computation.87 | convolution fusion | flops 1090519040 | bytes 19955712 | tf_op jit(solution)/shard_map/hck,hke->hce/dot_general | solution.py:25
  99.9 3.8 convolution_add_fusion
  105.6 5.8 %all-gather.10.cloned.1.call-done = bf16[512,2048]{1,0:T(8,128)(2,1)} async-done(((bf16[512,1024]{1,0:T(8,128)(2,1)}), bf16[512,2048]{1,0:T(8,128)(2,1)}) %all-gather.10.cloned.1.call-update) | async-done | bytes 2097168 | tf_op jit(solution)/shard_map/all_gather | solution.py:71
  111.4 24.2 %multiply_convert_fusion.2 = (bf16[1024,2048]{1,0:T(8,128)(2,1)}, f32[1024,2048]{1,0:T(8,128)}, f32[1024,2048]{1,0:T(8,128)}) fusion(bf16[512,2048]{1,0:T(8,128)(2,1)} %all-gather.10.cloned.1.call-done, f32[1024,512]{0,1:T(8,128)S(1)} %get-tuple-element.77, f32[512]{0:T(512)S(1)} %bitcast.179, f32[512]{0:T(512)S(1)} %bitcast.172, f32[1024]{0:T(1024)S(1)} %fusion.63, ...), kind=kOutput, calls=%fused_computation.10 | convolution fusion | flops 2286419968 | bytes 25178112 | tf_op jit(solution)/shard_map/ld,df->lf/dot_general | solution.py:25
  135.6 10.4 %all-gather.12.cloned.1.call-done = bf16[2048,512]{1,0:T(8,128)(2,1)} async-done(((bf16[1024,512]{1,0:T(8,128)(2,1)}), bf16[2048,512]{1,0:T(8,128)(2,1)}) %all-gather.12.cloned.1.call-update) | async-done | bytes 2097168 | tf_op jit(solution)/shard_map/all_gather | solution.py:72
  145.9 9.1 %add_convert_fusion.1 = bf16[1024,2048]{1,0:T(8,128)(2,1)S(1)} fusion(f32[1024,2048]{1,0:T(8,128)} %get-tuple-element.60, f32[1024,2048]{1,0:T(8,128)} %get-tuple-element.78, bf16[1024,512]{1,0:T(8,128)(2,1)S(1)} %copy-done.24, bf16[2048,512]{1,0:T(8,128)(2,1)} %all-gather.12.cloned.1.call-done), kind=kOutput, calls=%fused_computation.9 | convolution fusion | flops 2176843776 | bytes 24117248 | tf_op jit(solution)/shard_map/ld,fd->lf/dot_general | solution.py:25
  155.1 3.8 convolution_convert_fusion.1
  166.7 9.3 %fusion = bf16[8,1024,1024]{2,1,0:T(8,128)(2,1)} fusion(f32[8,1024]{1,0:T(8,128)S(1)} %bitcast.166, pred[1024,1024]{1,0:T(8,128)(4,1)S(1)} %copy-done.26, bf16[8,1024,64]{1,2,0:T(8,128)(2,1)S(1)} %get-tuple-element.67, bf16[8,1024,64]{1,2,0:T(8,128)(2,1)S(1)} %bitcast.142), kind=kOutput, calls=%fused_computation.2 | convolution fusion | flops 1098907648 | bytes 19955712 | tf_op jit(solution)/shard_map/hce,hke->hck/dot_general | solution.py:25
  176.0 12.5 %fusion.87 = f32[8,1024,256]{1,2,0:T(8,128)} fusion(bf16[8,1024,256]{1,2,0:T(8,128)(2,1)S(1)} %copy-done.2, bf16[8,1024,1024]{2,1,0:T(8,128)(2,1)} %fusion), kind=kOutput, calls=%fused_computation.162 | convolution fusion | flops 4294967296 | bytes 29360128 | tf_op jit(solution)/shard_map/hck,hcm->hkm/dot_general | solution.py:25
  188.5 11.6 %fusion.85 = f32[8,1024,256]{1,2,0:T(8,128)} fusion(bf16[8,1024,1024]{2,1,0:T(8,128)(2,1)} %fusion, bf16[8,1024,256]{1,2,0:T(8,128)(2,1)} %copy-done.3), kind=kOutput, calls=%fused_computation.160 | convolution fusion | flops 4294967296 | bytes 29360128 | tf_op jit(solution)/shard_map/hck,hkm->hcm/dot_general | solution.py:25
  200.1 6.3 %fusion.17 = bf16[512,2048]{0,1:T(8,128)(2,1)} fusion(bf16[1024,2048]{1,0:T(8,128)(2,1)} %get-tuple-element.59, bf16[1024,512]{1,0:T(8,128)(2,1)} %param.12), kind=kOutput, calls=%fused_computation.47 | convolution fusion | flops 2148532224 | bytes 7340032 | tf_op jit(solution)/shard_map/ld,lf->df/dot_general | solution.py:25
  209.0 7.9 %fusion.82 = (f32[8,1024]{1,0:T(8,128)S(1)}, f32[8,1024,256]{1,2,0:T(8,128)S(1)}) fusion(f32[8,1024]{1,0:T(8,128)S(1)} %broadcast_multiply_fusion.1, f32[8,1024,256]{1,2,0:T(8,128)} %get-tuple-element.73, f32[8,1024,256]{1,2,0:T(8,128)} %fusion.85, bf16[8,256,65]{1,0,2:T(8,128)(2,1)S(1)} %fusion.29, bf16[8,1024,1]{1,2,0:T(2,128)(2,1)S(1)} %get-tuple-element.55, ...), kind=kOutput, calls=%fused_computation.157 | convolution fusion | flops 287334400 | bytes 26562560 | tf_op jit(solution)/shard_map/hce,hme->hcm/dot_general | solution.py:25
  220.6 3.9 copy.147
  224.5 4.5 %convert_element_type.180 = bf16[16,32,1,2,1024]{4,3,1,0,2:T(2,128)(2,1)} reshape(bf16[512,2048]{1,0:T(8,128)(2,1)} %copy.147) | data formatting | bytes 4194304 | tf_op jit(solution)/shard_map/convert_element_type | solution.py:136
  232.5 4.5 %convert_element_type.175 = bf16[16,32,1,2,1024]{4,3,1,0,2:T(2,128)(2,1)} reshape(bf16[512,2048]{1,0:T(8,128)(2,1)} %convolution_convert_fusion.1) | data formatting | bytes 4194304 | tf_op jit(solution)/shard_map/convert_element_type | solution.py:136
  237.0 3.6 copy.146
  242.9 10.4 %fusion.88 = f32[8,1024,64]{1,2,0:T(8,128)} fusion(bf16[8,1024,64]{1,2,0:T(8,128)(2,1)} %copy-done.16, bf16[8,1024,1024]{2,1,0:T(8,128)(2,1)} %select_convert_fusion), kind=kOutput, calls=%fused_computation.163 | convolution fusion | flops 1073741824 | bytes 19922944 | tf_op jit(solution)/shard_map/hck,hce->hke/dot_general | solution.py:25
  254.8 4.8 %add_convert_fusion.2 = bf16[8,1024,64]{1,2,0:T(8,128)(2,1)} fusion(f32[8,1024,64]{1,2,0:T(8,128)} %fusion.88, bf16[8,1024,256]{1,2,0:T(8,128)(2,1)} %copy-done.3, bf16[8,256,65]{1,2,0:T(8,128)(2,1)S(1)} %copy.178), kind=kOutput, calls=%fused_computation.63 | convolution fusion | flops 269484032 | bytes 7602176 | tf_op jit(solution)/shard_map/hkm,hme->hke/dot_general | solution.py:25
  261.9 7.4 %fusion.81 = (f32[8,1024]{1,0:T(8,128)S(1)}, f32[8,1024,256]{1,2,0:T(8,128)S(1)}) fusion(f32[8,1024]{1,0:T(8,128)S(1)} %copy-done.34, f32[8,1024,256]{1,2,0:T(8,128)} %get-tuple-element.75, f32[8,1024,256]{1,2,0:T(8,128)} %fusion.87, bf16[8,1024,64]{1,2,0:T(8,128)(2,1)S(1)} %bitcast.143, bf16[8,256,65]{1,0,2:T(8,128)(2,1)S(1)} %fusion.28), kind=kOutput, calls=%fused_computation.156 | convolution fusion | flops 285204480 | bytes 26546176 | tf_op jit(solution)/shard_map/hke,hme->hkm/dot_general | solution.py:25
  273.9 4.9 %convolution_convert_fusion.2 = bf16[512,3,512]{2,0,1:T(8,128)(2,1)} fusion(bf16[1,1024,512]{2,1,0:T(8,128)(2,1)} %copy.142, bf16[1,1024,512]{2,1,0:T(8,128)(2,1)} %copy.141, bf16[1,1024,512]{2,1,0:T(8,128)(2,1)} %copy.140, bf16[1024,512]{0,1:T(8,128)(2,1)S(1)} %copy-done.1, f32[512]{0:T(512)S(1)} %bitcast.178, f32[512]{0:T(512)S(1)} %bitcast.168, ...), kind=kOutput, calls=%fused_computation.73 | convolution fusion | flops 1623982080 | bytes 5779456 | tf_op jit(solution)/shard_map/ld,cle->dce/dot_general | solution.py:25
  282.3 4.1 copy.183
  286.4 5.3 %convert_element_type.169 = bf16[32,32,768]{2,1,0:T(8,128)(2,1)} reshape(bf16[16,2,32,3,256]{4,3,2,1,0:T(4,128)(2,1)} %bitcast.150) | data formatting | bytes 3145728 | tf_op jit(solution)/shard_map/convert_element_type | solution.py:136
  291.8 6.5 %pad_maximum_fusion = bf16[32,32,3072]{2,1,0:T(8,128)(2,1)} fusion(bf16[32,32,1024]{2,1,0:T(8,128)(2,1)} %bitcast.153, bf16[32,32,1024]{2,1,0:T(8,128)(2,1)} %bitcast.154, bf16[32,32,256]{2,1,0:T(8,128)(2,1)} %bitcast.161, bf16[32,32,768]{2,1,0:T(8,128)(2,1)} %convert_element_type.169), kind=kLoop, calls=%fused_computation.28 | loop fusion | flops 25165824 | bytes 12582912 | tf_op jit(solution)/shard_map/concatenate | solution.py:138
  298.2 6.6 %convolution_add_fusion.1 = f32[1024,512]{0,1:T(8,128)} fusion(f32[1024,512]{0,1:T(8,128)S(1)} %get-tuple-element.77, bf16[1024,2048]{1,0:T(8,128)(2,1)} %get-tuple-element.59, bf16[2048,512]{1,0:T(8,128)(2,1)} %all-gather.12.cloned.1.call-done), kind=kOutput, calls=%fused_computation.75 | convolution fusion | flops 2148007936 | bytes 10485760 | tf_op jit(solution)/shard_map/lf,fd->ld/dot_general | solution.py:25
  307.9 4.9 %fusion.83 = (f32[512]{0:T(512)S(1)}, f32[1024,512]{1,0:T(8,128)}) fusion(bf16[512,3,512]{0,2,1:T(8,128)(2,1)} %all-gather.8.cloned.1.call-done, bf16[1,1024,512]{2,1,0:T(8,128)(2,1)S(1)} %copy-done.28, bf16[1,1024,512]{2,1,0:T(8,128)(2,1)} %copy.141, bf16[1,1024,512]{2,1,0:T(8,128)(2,1)S(1)} %copy-done.27), kind=kOutput, calls=%fused_computation.158 | convolution fusion | flops 1614282240 | bytes 6817792 | tf_op jit(solution)/shard_map/cle,dce->ld/dot_general | solution.py:25
  322.1 40.8 %all-reduce.1 = (f32[2,512]{1,0:T(2,128)}, f32[2,512]{1,0:T(2,128)}) all-reduce(f32[2,512]{1,0:T(2,128)S(1)} %get-tuple-element.86, f32[2,512]{1,0:T(2,128)S(1)} %get-tuple-element.87), channel_id=1, replica_groups=mesh['dp'=16,'tensor'=2] {'dp','tensor'}, use_global_device_ids=true, to_apply=%region_18.19 | all-reduce | flops 2048 | bytes 16384 | tf_op jit(solution)/shard_map/psum | solution.py:145
  362.9 50.9 %reduce-scatter.2.cloned.1.call-done = bf16[1,32,3072]{2,1,0:T(8,128)(2,1)} async-done(((bf16[32,32,3072]{2,1,0:T(8,128)(2,1)}), bf16[1,32,3072]{2,1,0:T(8,128)(2,1)}) %reduce-scatter.2.cloned.1.call-update) | async-done | bytes 196624 | tf_op jit(solution)/shard_map/reduce_scatter | solution.py:141
  (189 shorter events, 69.0 us)
Async XLA Ops:
  7.2 32.9 %all-gather.8.cloned.1.call-start = ((), (), s32[]{:S(2)}) async-start(), calls=%async_computation.1 | async-start | bytes 2359296 | tf_op jit(solution)/shard_map/all_gather | solution.py:69
  9.6 88.9 %all-gather.14.cloned.1.call-start = ((), (), s32[]{:S(2)}) async-start(), calls=%async_computation.5 | async-start | bytes 1597440 | tf_op jit(solution)/shard_map/all_gather | solution.py:55
  11.1 93.0 %copy-start = (bf16[1024,512]{0,1:T(8,128)(2,1)}, bf16[1024,512]{0,1:T(8,128)(2,1)S(1)}, u32[]{:S(2)}) copy-start(bf16[1024,512]{0,1:T(8,128)(2,1)S(1)} %copy.122) | copy-start | bytes 3145732
  11.3 28.8 %copy-start.36 = (f32[1024]{0:T(1024)}, f32[1024]{0:T(1024)S(1)}, u32[]{:S(2)}) copy-start(f32[1024]{0:T(1024)S(1)} %broadcast_multiply_fusion.3) | copy-start | bytes 12292
  11.7 59.2 %copy-start.44 = (pred[8]{0:T(512)(128)(4,1)}, pred[8]{0:T(512)(128)(4,1)S(1)}, u32[]{:S(2)}) copy-start(pred[8]{0:T(512)(128)(4,1)S(1)} %broadcast_compare_fusion) | copy-start | bytes 28
  11.7 28.4 %copy-start.42 = (f32[1,512]{1,0:T(1,128)}, f32[1,512]{1,0:T(1,128)S(1)}, u32[]{:S(2)}) copy-start(f32[1,512]{1,0:T(1,128)S(1)} %get-tuple-element.69) | copy-start | bytes 6148
  12.2 31.2 %copy-start.48 = (f32[1,512]{1,0:T(1,128)}, f32[1,512]{1,0:T(1,128)S(1)}, u32[]{:S(2)}) copy-start(f32[1,512]{1,0:T(1,128)S(1)} %get-tuple-element.71) | copy-start | bytes 6148
  12.2 27.8 %copy-start.38 = (f32[1024]{0:T(1024)}, f32[1024]{0:T(1024)S(1)}, u32[]{:S(2)}) copy-start(f32[1024]{0:T(1024)S(1)} %fusion.62) | copy-start | bytes 12292
  43.9 4.9 %copy-start.10 = (bf16[1,1024,512]{1,2,0:T(8,128)(2,1)}, bf16[1,1024,512]{1,2,0:T(8,128)(2,1)S(1)}, u32[]{:S(2)}) copy-start(bf16[1,1024,512]{1,2,0:T(8,128)(2,1)S(1)} %get-tuple-element.62) | copy-start | bytes 3145732
  43.9 27.0 %copy-start.12 = (bf16[1,1024,512]{1,2,0:T(8,128)(2,1)}, bf16[1,1024,512]{1,2,0:T(8,128)(2,1)S(1)}, u32[]{:S(2)}) copy-start(bf16[1,1024,512]{1,2,0:T(8,128)(2,1)S(1)} %get-tuple-element.63) | copy-start | bytes 3145732
  43.9 44.5 %copy-start.8 = (bf16[1,1024,512]{1,2,0:T(8,128)(2,1)}, bf16[1,1024,512]{1,2,0:T(8,128)(2,1)S(1)}, u32[]{:S(2)}) copy-start(bf16[1,1024,512]{1,2,0:T(8,128)(2,1)S(1)} %get-tuple-element.61) | copy-start | bytes 3145732
  50.8 5.6 %copy-start.35 = (bf16[256,512]{1,0:T(8,128)(2,1)S(1)}, bf16[256,512]{1,0:T(8,128)(2,1)}, u32[]{:S(2)}) copy-start(bf16[256,512]{1,0:T(8,128)(2,1)} %param.14) | copy-start | bytes 786436
  53.2 58.2 %all-gather.10.cloned.1.call-start = ((), (), s32[]{:S(2)}) async-start(), calls=%async_computation.2 | async-start | bytes 3145728 | tf_op jit(solution)/shard_map/all_gather | solution.py:71
  53.9 92.0 %all-gather.12.cloned.1.call-start = ((), (), s32[]{:S(2)}) async-start(), calls=%async_computation.3 | async-start | bytes 3145728 | tf_op jit(solution)/shard_map/all_gather | solution.py:72
  54.5 198.8 %all-gather.16.cloned.1.call-start = ((), (), s32[]{:S(2)}) async-start(), calls=%async_computation.6 | async-start | bytes 1597440 | tf_op jit(solution)/shard_map/all_gather | solution.py:55
  70.9 5.7 %copy-start.25 = (pred[1024,1024]{1,0:T(8,128)(4,1)S(1)}, pred[1024,1024]{1,0:T(8,128)(4,1)}, u32[]{:S(2)}) copy-start(pred[1024,1024]{1,0:T(8,128)(4,1)} %iota_compare_fusion) | copy-start | bytes 3145732
  111.4 34.5 %copy-start.24 = (bf16[1024,512]{1,0:T(8,128)(2,1)S(1)}, bf16[1024,512]{1,0:T(8,128)(2,1)}, u32[]{:S(2)}) copy-start(bf16[1024,512]{1,0:T(8,128)(2,1)} %param.12) | copy-start | bytes 3145732
  166.5 9.5 %copy-start.16 = (bf16[8,1024,64]{1,2,0:T(8,128)(2,1)}, bf16[8,1024,64]{1,2,0:T(8,128)(2,1)S(1)}, u32[]{:S(2)}) copy-start(bf16[8,1024,64]{1,2,0:T(8,128)(2,1)S(1)} %get-tuple-element.67) | copy-start | bytes 3145732
  166.7 9.3 %copy-start.2 = (bf16[8,1024,256]{1,2,0:T(8,128)(2,1)S(1)}, bf16[8,1024,256]{1,2,0:T(8,128)(2,1)}, u32[]{:S(2)}) copy-start(bf16[8,1024,256]{1,2,0:T(8,128)(2,1)} %get-tuple-element.72) | copy-start | bytes 12582916
  200.1 6.3 %copy-start.17 = (bf16[8,1024,64]{1,2,0:T(8,128)(2,1)S(1)}, bf16[8,1024,64]{1,2,0:T(8,128)(2,1)}, u32[]{:S(2)}) copy-start(bf16[8,1024,64]{1,2,0:T(8,128)(2,1)} %copy-done.16) | copy-start | bytes 3145732
  208.9 204.9 %reduce-scatter.2.cloned.1.call-start = ((), (), s32[]{:S(2)}) async-start(), calls=%async_computation.4 | async-start | bytes 6488064 | tf_op jit(solution)/shard_map/reduce_scatter | solution.py:141
  208.9 8.0 %copy-start.13 = (bf16[1,1024,512]{1,2,0:T(8,128)(2,1)S(1)}, bf16[1,1024,512]{1,2,0:T(8,128)(2,1)}, u32[]{:S(2)}) copy-start(bf16[1,1024,512]{1,2,0:T(8,128)(2,1)} %copy-done.12) | copy-start | bytes 3145732
  208.9 8.0 %copy-start.30 = (bf16[64,256]{1,0:T(8,128)(2,1)S(1)}, bf16[64,256]{1,0:T(8,128)(2,1)}, u32[]{:S(2)}) copy-start(bf16[64,256]{1,0:T(8,128)(2,1)} %param.20) | copy-start | bytes 98308
  208.9 8.0 %copy-start.32 = (bf16[64,256]{1,0:T(8,128)(2,1)S(1)}, bf16[64,256]{1,0:T(8,128)(2,1)}, u32[]{:S(2)}) copy-start(bf16[64,256]{1,0:T(8,128)(2,1)} %param.19) | copy-start | bytes 98308
  209.0 8.0 %copy-start.45 = (pred[8]{0:T(512)(128)(4,1)S(1)}, pred[8]{0:T(512)(128)(4,1)}, u32[]{:S(2)}) copy-start(pred[8]{0:T(512)(128)(4,1)} %copy-done.44) | copy-start | bytes 28
  242.9 10.5 %copy-start.51 = (pred[2]{0:T(512)(128)(4,1)S(1)}, pred[2]{0:T(512)(128)(4,1)}, u32[]{:S(2)}) copy-start(pred[2]{0:T(512)(128)(4,1)} %iota_compare_fusion.1) | copy-start | bytes 10
  254.8 7.1 %copy-start.34 = (f32[8,1024]{1,0:T(8,128)S(1)}, f32[8,1024]{1,0:T(8,128)}, u32[]{:S(2)}) copy-start(f32[8,1024]{1,0:T(8,128)} %copy-done.33) | copy-start | bytes 98308
  261.9 7.4 %copy-start.11 = (bf16[1,1024,512]{1,2,0:T(8,128)(2,1)S(1)}, bf16[1,1024,512]{1,2,0:T(8,128)(2,1)}, u32[]{:S(2)}) copy-start(bf16[1,1024,512]{1,2,0:T(8,128)(2,1)} %copy-done.10) | copy-start | bytes 3145732
  269.3 4.6 %copy-start.1 = (bf16[1024,512]{0,1:T(8,128)(2,1)S(1)}, bf16[1024,512]{0,1:T(8,128)(2,1)}, u32[]{:S(2)}) copy-start(bf16[1024,512]{0,1:T(8,128)(2,1)} %copy-done) | copy-start | bytes 3145732
  269.3 4.6 %copy-start.37 = (f32[1024]{0:T(1024)S(1)}, f32[1024]{0:T(1024)}, u32[]{:S(2)}) copy-start(f32[1024]{0:T(1024)} %copy-done.36) | copy-start | bytes 12292
  269.3 4.6 %copy-start.39 = (f32[1024]{0:T(1024)S(1)}, f32[1024]{0:T(1024)}, u32[]{:S(2)}) copy-start(f32[1024]{0:T(1024)} %copy-done.38) | copy-start | bytes 12292
  269.3 4.6 %copy-start.43 = (f32[1,512]{1,0:T(1,128)S(1)}, f32[1,512]{1,0:T(1,128)}, u32[]{:S(2)}) copy-start(f32[1,512]{1,0:T(1,128)} %copy-done.42) | copy-start | bytes 6148
  (28 other events, 71.8 us)
Sparse Core Ops, SparseCore 0:
  10.1 29.8 all-gather.7
  53.3 23.3 all-gather.13
  78.3 33.0 all-gather.9
  112.8 33.0 all-gather.11
  209.0 21.4 all-gather.15
  298.4 115.3 reduce-scatter.1

commit v2 on v1

--- a/solution.py
+++ b/solution.py
@@ -1,6 +1,8 @@
 import jax
 import jax.numpy as jnp
 from jax import lax
+from jax.experimental import pallas as pl
+from jax.experimental.pallas import tpu as pltpu
 from jax.sharding import PartitionSpec as P
 
 HEAD_DIM = 64
@@ -8,6 +10,798 @@
 EPS = 1e-05
 F32 = jnp.float32
 BF16 = jnp.bfloat16
+FACTOR = HEAD_DIM ** (-0.25)
+ROWS, WIDE, TILE, FF = 1024, 512, 256, 2048
+TILES = ROWS // TILE
+PAIRS = 4
+
+
+def nn(a, b):
+    return lax.dot_general(a, b, (((1,), (0,)), ((), ())), preferred_element_type=F32)
+
+
+def nt(a, b):
+    return lax.dot_general(a, b, (((1,), (1,)), ((), ())), preferred_element_type=F32)
+
+
+def tn(a, b):
+    return lax.dot_general(a, b, (((0,), (0,)), ((), ())), preferred_element_type=F32)
+
+
+def iota(shape, dim):
+    return lax.broadcasted_iota(jnp.int32, shape, dim)
+
+
+def row_tile(t):
+    return pl.ds(pl.multiple_of(t * TILE, TILE), TILE)
+
+
+def lane_tile(j, width=128):
+    return pl.ds(pl.multiple_of(j * width, width), width)
+
+
+def loop(n, body):
+    lax.fori_loop(0, n, lambda i, c: (body(i), c)[1], 0)
+
+
+def of_head(shape, dim, head):
+    return (iota(shape, dim) & HEAD_DIM) == head * HEAD_DIM
+
+
+def centre(v):
+    mean = jnp.mean(v, axis=-1, keepdims=True)
+    off = v - mean
+    rstd = lax.rsqrt(jnp.mean(off * off, axis=-1, keepdims=True) + EPS)
+    return off * rstd, rstd
+
+
+def centre_back(grad, hat, rstd, gain):
+    scaled = grad * gain
+    first = jnp.mean(scaled, axis=-1, keepdims=True)
+    second = jnp.mean(scaled * hat, axis=-1, keepdims=True)
+    return rstd * (scaled - first - hat * second)
+
+
+def gelu_and_slope(u):
+    bell = jnp.exp(-0.5 * u * u)
+    t = 1.0 / (1.0 + (0.3275911 * 0.7071067811865476) * jnp.abs(u))
+    poly = 0.5 * 1.061405429
+    for c in (-1.453152027, 1.421413741, -0.284496736, 0.254829592):
+        poly = poly * t + 0.5 * c
+    tail = poly * t * bell
+    cdf = jnp.where(u >= 0, 1.0 - tail, tail)
+    return u * cdf, cdf + (0.3989422804014327 * u) * bell
+
+
+def features_of(rows, wf):
+    wide = rows.astype(F32)
+    both = jnp.concatenate([rows, ((0.5 * FACTOR) * wide * wide).astype(BF16)], axis=1)
+    return (jnp.exp(FACTOR * nn(both, wf)) * FEATURES ** (-0.5)).astype(BF16)
+
+
+def features_back(rows, wf, weighted):
+    through = nt(weighted, wf)
+    half = 2 * HEAD_DIM
+    return FACTOR * through[:, :half] + (FACTOR * FACTOR) * through[:, half:] * rows.astype(F32)
+
+
+def merge_heads(state):
+    own = of_head((state.shape[0], FEATURES), 0, 0)
+    return jnp.where(own, state[:, :FEATURES], state[:, FEATURES:])
+
+
+class Phases:
+    def __init__(self, **refs):
+        self.__dict__.update(refs)
+
+    def set_up(self):
+        self.vx[:, :, 128:] = jnp.ones((PAIRS, ROWS, 128), BF16)
+        fresh, last = self.fresh[...], self.last[...]
+        zero = jnp.zeros((HEAD_DIM, FEATURES), BF16)
+        minus = jnp.full((HEAD_DIM, FEATURES), -1.0, BF16)
+        for j in range(PAIRS):
+            for head in range(2):
+                flag = (self.flags[2 * j + head] == 1).astype(F32)
+                omega = (flag * fresh.astype(F32) + (1.0 - flag) * last.astype(F32)).astype(BF16)
+                for lower, block in ((0, omega), (128, minus)):
+                    for other in range(2):
+                        at = pl.ds(lower + head * HEAD_DIM, HEAD_DIM)
+                        col = pl.ds(other * FEATURES, FEATURES)
+                        self.wf[j, at, col] = block if other == head else zero
+        self.small[...] = jnp.zeros(self.small.shape, F32)
+
+    def norm1(self):
+        def body(t):
+            hat, _ = centre(self.tokens[row_tile(t), :].astype(F32))
+            self.n1[row_tile(t), :] = (hat * self.gains[0:1, :] + self.shifts[0:1, :]).astype(BF16)
+
+        loop(TILES, body)
+
+    def project(self, hh):
+        for jj in range(2):
+            self.run[jj] = jnp.zeros((TILE, FEATURES), F32)
+
+        def body(t):
+            rows = self.n1[row_tile(t), :]
+            parts = [
+                nn(rows, self.wqkv[hh, :, c * 256 : (c + 1) * 256]).astype(BF16) for c in range(3)
+            ]
+            for jj in range(2):
+                j = 2 * hh + jj
+                q, k, v = (p[:, jj * 128 : (jj + 1) * 128] for p in parts)
+                self.q[j, row_tile(t), :] = q
+                self.k[j, row_tile(t), :] = k
+                self.vx[j, row_tile(t), 0:128] = v
+                wf = self.wf[j]
+                self.phi_q[j, row_tile(t), :] = features_of(q, wf)
+                phi_k = features_of(k, wf)
+                self.phi_k[j, row_tile(t), :] = phi_k
+                state = merge_heads(tn(self.vx[j, row_tile(t), :], phi_k))
+                self.zt[j * TILES + t] = state.astype(BF16)
+                self.run[jj] += state
+
+        loop(TILES, body)
+        for jj in range(2):
+            self.pack(self.zsend, 2 * hh + jj, self.run.at[jj], False)
+
+    def pack(self, out, j, state, gradient):
+        first, second = state[128:136, :], state[192:200, :]
+        if gradient:
+            first = 0.5 * (first + state[160:168, :])
+            second = 0.5 * (second + state[224:232, :])
+        out[j, 0:128, :] = state[0:128, :].astype(BF16)
+        out[j, 128:136, :] = first.astype(BF16)
+        out[j, 136:144, :] = second.astype(BF16)
+
+    def unpack(self, packed):
+        low = packed.astype(F32)
+        sums = [jnp.broadcast_to(low[r : r + 1], (HEAD_DIM, FEATURES)) for r in (128, 136)]
+        return jnp.concatenate([low[0:128], *sums], axis=0)
+
+    def attend(self, hh, start):
+        for jj in range(2):
+            j = 2 * hh + jj
+            self.run[0] = start(j)
+
+            def body(t, j=j):
+                at = row_tile(t)
+                before = self.run[0]
+                low = before.astype(BF16)
+                self.run[0] = before + self.zt[j * TILES + t].astype(F32)
+                self.zt[j * TILES + t] = low
+                vx = self.vx[j, at, :]
+                both = []
+                for head in range(2):
+                    f = slice(head * FEATURES, (head + 1) * FEATURES)
+                    phi_q, phi_k = self.phi_q[j, at, f], self.phi_k[j, at, f]
+                    s = nt(phi_q, phi_k)
+                    s = jnp.where(iota(s.shape, 1) <= iota(s.shape, 0), s, 0.0).astype(BF16)
+                    both.append(nn(s, vx) + nt(phi_q, low))
+                r = jnp.where(of_head(both[0].shape, 1, 0), both[0], both[1])
+                inverse = 1.0 / r[:, 128:]
+                self.a[at, lane_tile(j)] = (r[:, :128] * inverse).astype(BF16)
+                self.inverse[j, at, :] = inverse
+
+            loop(TILES, body)
+
+    def norm2(self):
+        def body(t):
+            at = row_tile(t)
+            w_out = self.wout[...].reshape(WIDE, WIDE)
+            h = self.tokens[at, :].astype(F32) + nn(self.a[at, :], w_out)
+            self.out[at, :] = h
+            hat, rstd = centre(h)
+            self.hat2[at, :] = hat.astype(BF16)
+            self.rstd2[at, :] = jnp.broadcast_to(rstd, (TILE, 128))
+            self.n2[at, :] = (hat * self.gains[1:2, :] + self.shifts[1:2, :]).astype(BF16)
+            self.grad[at, :] = jnp.zeros((TILE, WIDE), F32)
+
+        loop(TILES, body)
+
+    def feed(self, slot):
+        def body(i):
+            t, p = lax.div(i, 2), lax.rem(i, 2)
+            at, cols = row_tile(t), lane_tile(p, 512)
+            w_up, w_down = self.wup[slot, :, cols], self.wdown[slot, cols, :]
+            g, slope = gelu_and_slope(nn(self.n2[at, :], w_up))
+            g = g.astype(BF16)
+            du = (slope * nt(self.cot[at, :], w_down)).astype(BF16)
+            self.g[t * 4 + slot * 2 + p] = g
+            self.du[t * 4 + slot * 2 + p] = du
+            self.out[at, :] += nn(g, w_down)
+            self.grad[at, :] += nt(du, w_up)
+
+        loop(2 * TILES, body)
+
+    def norm2_back(self):
+        def body(t):
+            at = row_tile(t)
+            grad, hat = self.grad[at, :], self.hat2[at, :].astype(F32)
+            self.small[1:2, :] += jnp.sum(grad * hat, axis=0, keepdims=True)
+            self.small[3:4, :] += jnp.sum(grad, axis=0, keepdims=True)
+            back = centre_back(grad, hat, self.rstd2[at, 0:1], self.gains[1:2, :])
+            dh = self.cot[at, :].astype(F32) + back
+            self.grad[at, :] = dh
+            self.dhb[at, :] = dh.astype(BF16)
+
+        loop(TILES, body)
+
+    def flip(self, source, out):
+        def body(t):
+            out[:, row_tile(t)] = source[row_tile(t), :].T
+
+        loop(TILES, body)
+
+    def weight_grad(self, xt, blocks, n_cols, store):
+        def body(c):
+            total = nn(xt[:, 0:TILE], blocks(0, c))
+            for t in range(1, TILES):
+                total = total + nn(xt[:, t * TILE : (t + 1) * TILE], blocks(t, c))
+            store(c, total)
+
+        loop(n_cols, body)
+
+    def attend_back_start(self):
+        def body(t):
+            at = row_tile(t)
+            w_out = self.wout[...].reshape(WIDE, WIDE)
+            da = nt(self.dhb[at, :], w_out)
+            o = self.a[at, :].astype(F32)
+            same = (iota((128, 128), 0) & HEAD_DIM) == (iota((128, 128), 1) & HEAD_DIM)
+            ones = jnp.where(same, 1.0, 0.0).astype(BF16)
+            high = (iota((TILE, 128), 1) & 32) == 0
+            for j in range(PAIRS):
+                lanes = slice(j * 128, (j + 1) * 128)
+                do, inverse = da[:, lanes], self.inverse[j, at, :]
+                dden = -nn((do * o[:, lanes]).astype(BF16), ones) * inverse
+                top = dden.astype(BF16)
+                rest = (dden - top.astype(F32)).astype(BF16)
+                self.dnx[j, at, 0:128] = (do * inverse).astype(BF16)
+                self.dnx[j, at, 128:] = jnp.where(high, top, rest) * jnp.asarray(1 / 32, BF16)
+
+        loop(TILES, body)
+
+    def sums_back(self, j):
+        self.run[0] = jnp.zeros((TILE, FEATURES), F32)
+
+        def body(t):
+            at = row_tile(t)
+            state = merge_heads(tn(self.dnx[j, at, :], self.phi_q[j, at, :]))
+            self.gt[j * TILES + t] = state.astype(BF16)
+            self.run[0] += state
+
+        loop(TILES, body)
+        self.pack(self.gsend, j, self.run.at[0], True)
+
+    def back_q(self, j):
+        def body(t):
+            at = row_tile(t)
+            dnx = self.dnx[j, at, :]
+            w = []
+            for head in range(2):
+                f = slice(head * FEATURES, (head + 1) * FEATURES)
+                own = jnp.where(of_head(dnx.shape, 1, head), dnx, jnp.zeros_like(dnx))
+                ds = nt(own, self.vx[j, at, :])
+                ds = jnp.where(iota(ds.shape, 1) <= iota(ds.shape, 0), ds, 0.0).astype(BF16)
+                dphi = nn(ds, self.phi_k[j, at, f]) + nn(own, self.zt[j * TILES + t])
+                w.append((dphi * self.phi_q[j, at, f].astype(F32)).astype(BF16))
+            dq = features_back(self.q[j, at, :], self.wf[j], jnp.concatenate(w, axis=1))
+            self.dqkv[0 * TILES + t, :, lane_tile(j)] = dq.astype(BF16)
+
+        loop(TILES, body)
+
+    def back_kv(self, j, start):
+        self.run[0] = start(j)
+
+        def body(i):
+            t = TILES - 1 - i
+            at = row_tile(t)
+            after = self.run[0]
+            low = after.astype(BF16)
+            self.run[0] = after + self.gt[j * TILES + t].astype(F32)
+            dnx, vx = self.dnx[j, at, :], self.vx[j, at, :]
+            w, dv = [], []
+            for head in range(2):
+                f = slice(head * FEATURES, (head + 1) * FEATURES)
+                phi_q, phi_k = self.phi_q[j, at, f], self.phi_k[j, at, f]
+                st = nt(phi_k, phi_q)
+                upper = iota(st.shape, 0) <= iota(st.shape, 1)
+                st = jnp.where(upper, st, 0.0).astype(BF16)
+                own = jnp.where(of_head(vx.shape, 1, head), vx, jnp.zeros_like(vx))
+                dst = nt(own, dnx)
+                dst = jnp.where(upper, dst, 0.0).astype(BF16)
+                dphi = nn(dst, phi_q) + nn(own, low)
+                w.append((dphi * phi_k.astype(F32)).astype(BF16))
+                dv.append(nn(st, dnx[:, 0:128]) + nt(phi_k, low[0:128]))
+            dk = features_back(self.k[j, at, :], self.wf[j], jnp.concatenate(w, axis=1))
+            self.dqkv[1 * TILES + t, :, lane_tile(j)] = dk.astype(BF16)
+            dv = jnp.where(of_head(dv[0].shape, 1, 0), dv[0], dv[1])
+            self.dqkv[2 * TILES + t, :, lane_tile(j)] = dv.astype(BF16)
+
+        loop(TILES, body)
+
+    def norm1_back(self):
+        def body(t):
+            at = row_tile(t)
+            grad = jnp.zeros((TILE, WIDE), F32)
+            for hh in range(2):
+                for c in range(3):
+                    part = self.dqkv[c * TILES + t, :, hh * 256 : (hh + 1) * 256]
+                    grad = grad + nt(part, self.wqkv[hh, :, c * 256 : (c + 1) * 256])
+            hat, rstd = centre(self.tokens[at, :].astype(F32))
+            self.small[0:1, :] += jnp.sum(grad * hat, axis=0, keepdims=True)
+            self.small[2:3, :] += jnp.sum(grad, axis=0, keepdims=True)
+            self.grad[at, :] += centre_back(grad, hat, rstd, self.gains[0:1, :])
+
+        loop(TILES, body)
+
+
+def work_buffers():
+    vmem = pltpu.VMEM
+    return dict(
+        n1=vmem((ROWS, WIDE), BF16),
+        q=vmem((PAIRS, ROWS, 128), BF16),
+        k=vmem((PAIRS, ROWS, 128), BF16),
+        vx=vmem((PAIRS, ROWS, 256), BF16),
+        phi_q=vmem((PAIRS, ROWS, 512), BF16),
+        phi_k=vmem((PAIRS, ROWS, 512), BF16),
+        zt=vmem((PAIRS * TILES, 256, 256), BF16),
+        gt=vmem((PAIRS * TILES, 256, 256), BF16),
+        run=vmem((2, 256, 256), F32),
+        wf=vmem((PAIRS, 256, 512), BF16),
+        a=vmem((ROWS, WIDE), BF16),
+        inverse=vmem((PAIRS, ROWS, 128), F32),
+        n2=vmem((ROWS, WIDE), BF16),
+        hat2=vmem((ROWS, WIDE), BF16),
+        rstd2=vmem((ROWS, 128), F32),
+        g=vmem((TILES * 4, 256, 512), BF16),
+        du=vmem((TILES * 4, 256, 512), BF16),
+        dhb=vmem((ROWS, WIDE), BF16),
+        dnx=vmem((PAIRS, ROWS, 256), BF16),
+        zsend=vmem((PAIRS, 144, 256), BF16),
+        gsend=vmem((PAIRS, 144, 256), BF16),
+        xt=vmem((WIDE, ROWS), BF16),
+        xt2=vmem((WIDE, ROWS), BF16),
+        small=vmem((4, WIDE), F32),
+    )
+
+
+MESH = pl.DeviceIdType.MESH
+OWNED = 1024
+
+
+class Links:
+    def __init__(self, deep, refs):
+        self.deep = deep
+        self.__dict__.update(refs)
+        self.dp, self.me = lax.axis_index("dp"), lax.axis_index("tensor")
+        self.core = lax.rem(self.dp, 2)
+        self.x = lax.rem(lax.div(self.dp, 2), 2)
+        self.z = lax.div(self.dp, 4)
+        self.block = WIDE // (4 * deep)
+
+    def place(self, axis, step=1):
+        dp, me = self.dp, self.me
+        if axis == "core":
+            return dict(dp=dp + 1 - 2 * self.core, tensor=me)
+        if axis == "x":
+            return dict(dp=dp + 2 - 4 * self.x, tensor=me)
+        if axis == "y":
+            return dict(dp=dp, tensor=1 - me)
+        return dict(dp=dp + 4 * (lax.rem(self.z + step, self.deep) - self.z), tensor=me)
+
+    def partners(self):
+        steps = [self.place("z", s) for s in range(1, self.deep)]
+        return [self.place(a) for a in ("core", "x", "y")] + steps
+
+    def greet(self):
+        barrier = pltpu.get_barrier_semaphore()
+        for where in self.partners():
+            pl.semaphore_signal(barrier, inc=1, device_id=where, device_id_type=MESH)
+
+    def met(self):
+        pl.semaphore_wait(pltpu.get_barrier_semaphore(), len(self.partners()))
+
+    def copy(self, source, target, sems, at, where):
+        return pltpu.make_async_remote_copy(
+            src_ref=source,
+            dst_ref=target,
+            send_sem=sems.at[2 * at],
+            recv_sem=sems.at[2 * at + 1],
+            device_id=where,
+            device_id_type=MESH,
+        )
+
+
+    def weight(self, i):
+        source = (self.wqkv_in, self.wout_in, self.wup_in, self.wdown_in)[i]
+        return source, (self.wqkv, self.wout, self.wup, self.wdown)[i], source.shape[0] // 2
+
+    def own_weight(self, i):
+        source, slots, _ = self.weight(i)
+        return pltpu.make_async_copy(source, slots.at[self.me], self.own_sems.at[i])
+
+    def weight_over(self, i):
+        source, slots, half = self.weight(i)
+        part = pl.ds(pl.multiple_of(self.core * half, half), half)
+        target = slots.at[self.me, part]
+        return self.copy(source.at[part], target, self.over_sems, i, self.place("y"))
+
+    def weight_along(self, i):
+        _, slots, half = self.weight(i)
+        part = pl.ds(pl.multiple_of(self.core * half, half), half)
+        held = slots.at[1 - self.me, part]
+        return self.copy(held, held, self.along_sems, i, self.place("core"))
+
+
+    def axes(self, seg):
+        return ("y", "x") if seg != 1 else ("x", "y")
+
+    def index(self, axis):
+        return self.me if axis == "y" else self.x
+
+    def stage(self, seg, depth):
+        grads = self.grads[seg]
+        if depth == 0:
+            source = grads.at[1 - self.core]
+            return self.copy(source, self.got[seg][0], self.sum_sems[seg], 0, self.place("core"))
+        axis = self.axes(seg)[depth - 1]
+        start, size = self.span(seg, depth, 1 - self.index(axis))
+        source = grads.at[self.core, pl.ds(pl.multiple_of(start, self.block), size)]
+        return self.copy(source, self.got[seg][depth], self.sum_sems[seg], depth, self.place(axis))
+
+    def span(self, seg, depth, last):
+        start, size = 0, WIDE
+        for i in range(depth):
+            size = size // 2
+            at = last if i == depth - 1 else self.index(self.axes(seg)[i])
+            start = start + at * size
+        return start, size
+
+    def mine(self, seg, depth):
+        if depth == 0:
+            return 0, WIDE
+        return self.span(seg, depth, self.index(self.axes(seg)[depth - 1]))
+
+    def start(self, seg, depth):
+        self.stage(seg, depth).start()
+
+    def finish(self, seg, depth):
+        self.stage(seg, depth).wait()
+        start, size = self.mine(seg, depth)
+        grads, got = self.grads[seg], self.got[seg][depth]
+        step = min(size, 64)
+
+        def body(i):
+            there = pl.ds(pl.multiple_of(i * step, step), step)
+            here = pl.ds(pl.multiple_of(start + i * step, step), step)
+            grads[self.core, here] = grads[self.core, here] + got[there]
+
+        loop(size // step, body)
+
+    def z_copy(self, seg, step):
+        start, _ = self.mine(seg, 2)
+        row = start + lax.rem(self.z + step, self.deep) * self.block
+        source = self.grads[seg].at[self.core, pl.ds(pl.multiple_of(row, self.block), self.block)]
+        target = self.got[seg][3].at[step - 1]
+        return self.copy(source, target, self.sum_sems[seg], 2 + step, self.place("z", step))
+
+    def start_z(self, seg):
+        for step in range(1, self.deep):
+            self.z_copy(seg, step).start()
+
+    def finish_z(self, seg, out):
+        start, _ = self.mine(seg, 2)
+        here = pl.ds(pl.multiple_of(start + self.z * self.block, self.block), self.block)
+        total = self.grads[seg][self.core, here].astype(F32)
+        for step in range(1, self.deep):
+            self.z_copy(seg, step).wait()
+            total = total + self.got[seg][3][step - 1].astype(F32)
+        out[...] = total
+
+
+    def small_sum(self, small, heard):
+        slot = 0
+        for axis in ("core", "y", "x"):
+            both = self.copy(small, heard.at[slot], self.small_sems, slot, self.place(axis))
+            both.start()
+            both.wait()
+            small[...] = small[...] + heard[slot]
+            slot += 1
+        copies = [
+            self.copy(small, heard.at[2 + s], self.small_sems, 2 + s, self.place("z", s))
+            for s in range(1, self.deep)
+        ]
+        for both in copies:
+            both.start()
+        for both in copies:
+            both.wait()
+        total = small[...]
+        for s in range(1, self.deep):
+            total = total + heard[2 + s]
+        return total
+
+
+def scatter(grads, deep, c_of):
+    block = WIDE // (4 * deep)
+
+    def store(c, total):
+        tensor, col = c_of(c)
+        low = total.astype(BF16)
+        for d in range(4 * deep):
+            core, x, z = d % 2, d // 2 % 2, d // 4
+            ref, flipped = grads
+            near, far = (x, tensor) if flipped else (tensor, x)
+            row = ((near * 2 + far) * deep + z) * block
+            here = pl.ds(pl.multiple_of(row, block), block)
+            ref[core, here, lane_tile(col, TILE)] = low[d * block : (d + 1) * block]
+
+    return store
+
+
+def layer_kernel(deep, names, *refs):
+    r = dict(zip(names, refs))
+    sends = r["sum_sems"]
+    links = Links(
+        deep,
+        dict(
+            r,
+            grads=(r["grads0"], r["grads1"], r["wup"]),
+            got=tuple(tuple(r[f"got{d}"].at[s] for d in range(4)) for s in range(3)),
+            sum_sems=tuple(sends.at[s] for s in range(3)),
+        ),
+    )
+    p = Phases(**r, dqkv=r["du"])
+    me = links.me
+    other = 1 - me
+
+    links.greet()
+    for i in range(4):
+        links.own_weight(i).start()
+    p.set_up()
+    links.met()
+    for i in range(2):
+        links.weight_over(i).start()
+    p.norm1()
+    links.own_weight(0).wait()
+    p.project(me)
+
+    def pairs_of(ref, hh):
+        return ref.at[pl.ds(2 * hh, 2)]
+
+    def sums_to(source, target, sems, at, hh):
+        return links.copy(pairs_of(source, hh), pairs_of(target, hh), sems, at, links.place("y"))
+
+    @pl.when(me == 0)
+    def _():
+        p.zgot[...] = jnp.zeros(p.zgot.shape, BF16)
+        sums_to(p.zsend, p.zgot, r["z_sems"], 0, 0).start()
+
+    @pl.when(me == 1)
+    def _():
+        p.ggot[...] = jnp.zeros(p.ggot.shape, BF16)
+
+    for i in range(2):
+        links.weight_over(i).wait()
+        links.weight_along(i).start()
+    links.weight_along(0).wait()
+    p.project(other)
+
+    @pl.when(me == 0)
+    def _():
+        sums_to(p.zsend, p.zgot, r["z_sems"], 1, 1).start()
+
+    for i in range(2, 4):
+        links.weight_over(i).start()
+
+    @pl.when(me == 1)
+    def _():
+        for hh in range(2):
+            sums_to(p.zsend, p.zgot, r["z_sems"], hh, hh).wait_recv()
+
+    for hh in (me, other):
+        p.attend(hh, lambda j: p.unpack(p.zgot[j]))
+
+    @pl.when(me == 0)
+    def _():
+        for hh in range(2):
+            sums_to(p.zsend, p.zgot, r["z_sems"], hh, hh).wait_send()
+
+    links.own_weight(1).wait()
+    links.weight_along(1).wait()
+    p.norm2()
+    links.own_weight(2).wait()
+    links.own_weight(3).wait()
+    p.feed(me)
+    for i in range(2, 4):
+        links.weight_over(i).wait()
+        links.weight_along(i).start()
+    for i in range(2, 4):
+        links.weight_along(i).wait()
+    p.feed(other)
+
+    p.norm2_back()
+    p.attend_back_start()
+    loop(PAIRS, p.sums_back)
+
+    def grad_sums():
+        return links.copy(p.gsend, p.ggot, r["g_sems"], 0, links.place("y"))
+
+    @pl.when(me == 1)
+    def _():
+        grad_sums().start()
+
+    def by_ff(c):
+        return lax.div(c, 4), lax.rem(c, 4)
+
+    def half_block(ref):
+        return lambda t, c: ref[t * 4 + lax.div(c, 2), :, lane_tile(lax.rem(c, 2), TILE)]
+
+    p.flip(p.n2, p.xt)
+    p.weight_grad(p.xt, half_block(p.du), 8, scatter((links.grads[0], False), deep, by_ff))
+    links.start(0, 0)
+    p.flip(p.cot, p.xt2)
+    p.weight_grad(p.xt2, half_block(p.g), 8, scatter((links.grads[1], True), deep, by_ff))
+    links.start(1, 0)
+    links.finish(0, 0)
+    links.start(0, 1)
+    p.flip(p.dhb, p.xt)
+    p.weight_grad(
+        p.xt,
+        lambda t, c: p.a[pl.ds(t * TILE, TILE), lane_tile(c, TILE)],
+        2,
+        scatter((links.grads[2], False), deep, lambda c: (c, 0)),
+    )
+    links.finish(1, 0)
+    links.start(1, 1)
+    return p, links, r
+
+
+def layer_rest(deep, p, links, r):
+    me = links.me
+    loop(2, p.back_q)
+    loop(2, lambda j: p.back_q(j + 2))
+    for seg in range(2):
+        links.finish(seg, 1)
+        links.start(seg, 2)
+
+    def grad_sums():
+        return links.copy(p.gsend, p.ggot, r["g_sems"], 0, links.place("y"))
+
+    @pl.when(me == 0)
+    def _():
+        grad_sums().wait_recv()
+
+    @pl.when(me == 1)
+    def _():
+        grad_sums().wait_send()
+
+    def back(j):
+        p.back_kv(j, lambda j: p.unpack(p.ggot[j]))
+
+    loop(2, back)
+    for seg in range(2):
+        links.finish(seg, 2)
+        links.start_z(seg)
+    loop(2, lambda j: back(j + 2))
+    p.flip(p.n1, p.xt2)
+    p.weight_grad(
+        p.xt2,
+        lambda t, c: p.dqkv[lax.div(c, 2) * TILES + t, :, lane_tile(lax.rem(c, 2), TILE)],
+        6,
+        scatter((links.grads[2], False), deep, lambda c: (lax.rem(c, 2), 1 + lax.div(c, 2))),
+    )
+    links.start(2, 0)
+    p.norm1_back()
+    links.finish(2, 0)
+    links.start(2, 1)
+    for seg in range(2):
+        links.finish_z(seg, p.owned.at[seg])
+    p.norms[...] = links.small_sum(p.small, p.heard)
+    links.finish(2, 1)
+    links.start(2, 2)
+    links.finish(2, 2)
+    links.start_z(2)
+    links.finish_z(2, p.owned.at[2])
+
+
+def layer_call(deep, tokens, cotangent, wqkv, wout, wup, wdown, gains, shifts, fresh, last, flags):
+    vmem, hbm = pltpu.VMEM, pl.ANY
+    block = WIDE // (4 * deep)
+    inputs = dict(
+        tokens=(tokens, vmem),
+        cot=(cotangent, vmem),
+        wqkv_in=(wqkv, hbm),
+        wout_in=(wout, hbm),
+        wup_in=(wup, hbm),
+        wdown_in=(wdown, hbm),
+        gains=(gains, vmem),
+        shifts=(shifts, vmem),
+        fresh=(fresh, vmem),
+        last=(last, vmem),
+        flags=(flags, pltpu.SMEM),
+    )
+    outputs = dict(
+        out=jax.ShapeDtypeStruct((ROWS, WIDE), F32),
+        grad=jax.ShapeDtypeStruct((ROWS, WIDE), F32),
+        owned=jax.ShapeDtypeStruct((3, block, OWNED), F32),
+        norms=jax.ShapeDtypeStruct((4, WIDE), F32),
+    )
+    dma = pltpu.SemaphoreType.DMA
+    scratch = dict(
+        work_buffers(),
+        wqkv=vmem((2, WIDE, 768), BF16),
+        wout=vmem((2, 256, WIDE), BF16),
+        wup=vmem((2, WIDE, 1024), BF16),
+        wdown=vmem((2, 1024, WIDE), BF16),
+        zgot=vmem((PAIRS, 144, 256), BF16),
+        ggot=vmem((PAIRS, 144, 256), BF16),
+        grads0=vmem((2, WIDE, OWNED), BF16),
+        grads1=vmem((2, WIDE, OWNED), BF16),
+        got0=vmem((3, WIDE, OWNED), BF16),
+        got1=vmem((3, WIDE // 2, OWNED), BF16),
+        got2=vmem((3, WIDE // 4, OWNED), BF16),
+        got3=vmem((3, deep - 1, block, OWNED), BF16),
+        heard=vmem((2 + deep, 4, WIDE), F32),
+        own_sems=dma((4,)),
+        over_sems=dma((8,)),
+        along_sems=dma((8,)),
+        z_sems=dma((4,)),
+        g_sems=dma((2,)),
+        sum_sems=dma((3, 2 * (2 + deep))),
+        small_sems=dma((2 * (2 + deep),)),
+    )
+    names = (*inputs, *outputs, *scratch)
+
+    def kernel(*refs):
+        layer_rest(deep, *layer_kernel(deep, names, *refs))
+
+    return pl.pallas_call(
+        kernel,
+        out_shape=tuple(outputs.values()),
+        in_specs=[pl.BlockSpec(memory_space=space) for _, space in inputs.values()],
+        out_specs=tuple(pl.BlockSpec(memory_space=vmem) for _ in outputs),
+        scratch_shapes=list(scratch.values()),
+        compiler_params=pltpu.CompilerParams(
+            collective_id=0, has_side_effects=True, vmem_limit_bytes=67043328
+        ),
+        name="layer",
+    )(*(array for array, _ in inputs.values()))
+
+
+def fused(
+    tokens, cotangent, w_qkv, w_out, w_up, w_down, gains, shifts, feat_fresh, feat_last, flags
+):
+    deep = lax.axis_size("dp") // 4
+    result, grad_tokens, owned, norms = layer_call(
+        deep,
+        tokens,
+        cotangent,
+        w_qkv.reshape(WIDE, 768),
+        w_out,
+        w_up,
+        w_down,
+        gains,
+        shifts,
+        feat_fresh,
+        feat_last,
+        flags,
+    )
+    rest = owned[2]
+    return (
+        result,
+        grad_tokens,
+        rest[:, 256:].reshape(-1, 3, 256),
+        rest[:, :256].T,
+        owned[0],
+        owned[1].T,
+        norms[:2],
+        norms[2:],
+    )
+
+
+def fits(mesh):
+    return mesh.shape["tensor"] == 2 and mesh.shape["dp"] % 4 == 0 and mesh.shape["dp"] <= 64
 
 
 def normalize(inputs, norm_gain, offset):
@@ -35,7 +829,7 @@
     return moved.reshape(moved.shape[0], -1)
 
 
-def features(inputs, projector):
+def plain_features(inputs, projector):
     factor = HEAD_DIM ** (-0.25)
     projected = mul("hlc,hcm->hlm", inputs, projector)
     wide_in = inputs.astype(F32)
@@ -43,7 +837,7 @@
     return jnp.exp(factor * projected - squares) * FEATURES ** (-0.5)
 
 
-def features_back(inputs, projector, expo, grad_phi):
+def plain_features_back(inputs, projector, expo, grad_phi):
     factor = HEAD_DIM ** (-0.25)
     grad_pre = grad_phi * expo
     grad_proj = (factor * grad_pre).astype(BF16)
@@ -77,7 +871,7 @@
     projector = jnp.where((flags == 1)[:, None, None], feat_fresh[None], feat_last[None])
     mixed = mul("ld,dce->cle", normed, w_qkv).astype(BF16)
     queries, keys, values = (split_heads(mixed[c]) for c in range(3))
-    expo_q, expo_k = features(queries, projector), features(keys, projector)
+    expo_q, expo_k = plain_features(queries, projector), plain_features(keys, projector)
     phi_q, phi_k = expo_q.astype(BF16), expo_k.astype(BF16)
     summed_values = with_sums(values)
     memory = from_others(mul("hkm,hke->hme", phi_k, summed_values), True).astype(BF16)
@@ -117,8 +911,8 @@
     grad_v = grad_v + mul("hkm,hme->hke", phi_k, grad_memory[..., :-1])
     grad_mixed = jnp.stack(
         [
-            join_heads(features_back(queries, projector, expo_q, grad_q)),
-            join_heads(features_back(keys, projector, expo_k, grad_k)),
+            join_heads(plain_features_back(queries, projector, expo_q, grad_q)),
+            join_heads(plain_features_back(keys, projector, expo_k, grad_k)),
             join_heads(grad_v),
         ]
     ).astype(BF16)
@@ -173,7 +967,7 @@
         P(),
     )
     return jax.shard_map(
-        plain,
+        fused if fits(mesh) else plain,
         mesh=mesh,
         in_specs=placed,
         out_specs=(

time: 430 us -> 159 us (0.37); the launches traced: 424 us -> 158 us
  matrix products: 176 us -> 0 us
  Pallas kernels: 0 us -> 146 us
  waiting for transfers between devices: 96.1 us -> 0 us
  blocking collectives: 52.8 us -> 0 us
  local copies, waits for them, and re-layouts: 64.1 us -> 11.5 us
  other arithmetic: 18.9 us -> 0 us
  between operations: 15.1 us -> 0.65 us
    dot_general x28 -> x0, matrix products: 176 us -> none  [mul(): return jnp.einsum(spec, *operands, preferred_element_type=F32)]
    pallas_call x0 -> x1, Pallas kernels: none -> 146 us  [layer_call(): pl.pallas_call(kernel, out_shape=tuple(outputs.values()), in_specs=[pl.Bl...]
    reduce_scatter x1 -> x0, waiting for transfers between devices: 50.9 us -> none  [plain(): lax.psum_scatter(packed, ('dp', 'tensor'), scatter_dimension=0, tiled=True)]
    all_gather x5 -> x0, waiting for transfers between devices: 44 us -> none  [the longest x1 27.8 us: plain(): w_qkv = lax.all_gather(w_qkv, 'tensor', axis=2, tiled=True)]
    psum x1 -> x0, blocking collectives: 40.8 us -> none  [plain(): lax.psum((jnp.stack([grad_gain1, grad_gain2]), jnp.stack([grad_shift1, gr...]
    convert_element_type x8 -> x0, local copies, waits for them, and re-layouts: 33 us -> none  [by_owner(): return moved.reshape(dp * tensor, wide // dp, -1).astype(BF16)]
    all_gather x1 -> x0, blocking collectives: 12 us -> none  [plain(): w_out = lax.all_gather(w_out, 'tensor', axis=0, tiled=True)]
    unnamed x115 -> x5, local copies, waits for them, and re-layouts: 17.7 us -> 5.96 us
  transfers between devices with their start and end apart: 6 -> 0, of which waited for: 4 -> 0; matrix products, arithmetic and copies ran while one was open for 31% -> 0% of each run, Pallas kernels for 0% -> 0%
where the time goes in v2:
time: 159 us; the launch traced here: 158 us
  Pallas kernels  146 us (92%)
  local copies, waits for them, and re-layouts  11.5 us (7%)
    pallas_call x1, Pallas kernels, layer_call(): pl.pallas_call(kernel, out_shape=tuple(outputs.values()), in_specs=[pl.Bl...  146 us
    unnamed x5, local copies, waits for them, and re-layouts  5.96 us

profile of v2, /device:TPU:0, one launch (start us, length us, event | category | flops | bytes accessed | tf_op | source)
XLA Modules:
  0.0 158.2 jit_solution(4838943327010350213)
XLA Ops:
  0.6 1.4 copy.21
  2.0 1.2 copy.22.refs_2_
  3.2 146.1 %layer.1 = (f32[1024,512]{1,0:T(8,128)}, f32[1024,512]{1,0:T(8,128)}, f32[3,32,1024]{2,1,0:T(8,128)}, f32[4,512]{1,0:T(4,128)}) custom-call(bf16[1024,512]{1,0:T(8,128)(2,1)} %refs_0_.1, bf16[1024,512]{1,0:T(8,128)(2,1)} %refs_1_.1, bf16[512,768]{1,0:T(8,128)(2,1)} %copy.22.refs_2_, bf16[256,512]{1,0:T(8,128)(2,1)} %refs_3_.1, bf16[512,1024]{1,0:T(8,128)(2,1)} %refs_4_.1, ...), custom_call_target="tpu_custom_call" | custom-call | tf_op jit(solution)/shard_map/layer/pallas_call | solution.py:759
  149.3 1.4 fusion
  150.7 1.8 %slice_bitcast_fusion = (f32[1024,32]{0,1:T(8,128)}, f32[32,1024]{1,0:T(8,128)}, f32[32,1024]{1,0:T(8,128)S(1)}) fusion(f32[3,32,1024]{2,1,0:T(8,128)} %get-tuple-element.14), kind=kLoop, calls=%fused_computation | loop fusion | bytes 786432 | tf_op jit(solution)/shard_map/transpose | solution.py:797
  152.4 0.6 slice_bitcast_fusion.3
  153.0 0.6 copy.26
  153.7 0.0 copy-start
  153.7 3.2 %copy.29 = f32[1024,512]{1,0:T(8,128)} copy(f32[1024,512]{1,0:T(8,128)} %get-tuple-element.45) | data formatting | bytes 4194304
  156.9 0.0 copy-done
  156.9 1.3 copy.30
  (1 shorter events, 0.0 us)
Async XLA Ops:
  153.7 3.2 %copy-start = (f32[1024,512]{1,0:T(8,128)S(1)}, f32[1024,512]{1,0:T(8,128)}, u32[]{:S(2)}) copy-start(f32[1024,512]{1,0:T(8,128)} %get-tuple-element.46) | copy-start | bytes 6291460

commit v3 on v2

--- a/solution.py
+++ b/solution.py
@@ -124,7 +124,7 @@
         def body(t):
             rows = self.n1[row_tile(t), :]
             parts = [
-                nn(rows, self.wqkv[hh, :, c * 256 : (c + 1) * 256]).astype(BF16) for c in range(3)
+                nn(rows, self.wqkv[hh, c]).astype(BF16) for c in range(3)
             ]
             for jj in range(2):
                 j = 2 * hh + jj
@@ -158,31 +158,45 @@
         sums = [jnp.broadcast_to(low[r : r + 1], (HEAD_DIM, FEATURES)) for r in (128, 136)]
         return jnp.concatenate([low[0:128], *sums], axis=0)
 
-    def attend(self, hh, start):
+    def attend_near(self, hh):
         for jj in range(2):
             j = 2 * hh + jj
-            self.run[0] = start(j)
 
             def body(t, j=j):
                 at = row_tile(t)
-                before = self.run[0]
-                low = before.astype(BF16)
-                self.run[0] = before + self.zt[j * TILES + t].astype(F32)
-                self.zt[j * TILES + t] = low
                 vx = self.vx[j, at, :]
                 both = []
                 for head in range(2):
                     f = slice(head * FEATURES, (head + 1) * FEATURES)
-                    phi_q, phi_k = self.phi_q[j, at, f], self.phi_k[j, at, f]
-                    s = nt(phi_q, phi_k)
+                    s = nt(self.phi_q[j, at, f], self.phi_k[j, at, f])
                     s = jnp.where(iota(s.shape, 1) <= iota(s.shape, 0), s, 0.0).astype(BF16)
-                    both.append(nn(s, vx) + nt(phi_q, low))
+                    both.append(nn(s, vx))
                 r = jnp.where(of_head(both[0].shape, 1, 0), both[0], both[1])
-                inverse = 1.0 / r[:, 128:]
-                self.a[at, lane_tile(j)] = (r[:, :128] * inverse).astype(BF16)
-                self.inverse[j, at, :] = inverse
+                self.out[at, lane_tile(j)] = r[:, :128]
+                self.grad[at, lane_tile(j)] = r[:, 128:]
 
             loop(TILES, body)
+
+    def attend_far(self, j, start):
+        self.run[0] = start(j)
+
+        def body(t):
+            at = row_tile(t)
+            before = self.run[0]
+            low = before.astype(BF16)
+            self.run[0] = before + self.zt[j * TILES + t].astype(F32)
+            self.zt[j * TILES + t] = low
+            both = [
+                nt(self.phi_q[j, at, head * FEATURES : (head + 1) * FEATURES], low)
+                for head in range(2)
+            ]
+            r = jnp.where(of_head(both[0].shape, 1, 0), both[0], both[1])
+            inverse = 1.0 / (r[:, 128:] + self.grad[at, lane_tile(j)])
+            num = r[:, :128] + self.out[at, lane_tile(j)]
+            self.a[at, lane_tile(j)] = (num * inverse).astype(BF16)
+            self.inverse[j, at, :] = inverse
+
+        loop(TILES, body)
 
     def norm2(self):
         def body(t):
@@ -198,8 +212,9 @@
 
         loop(TILES, body)
 
-    def feed(self, slot):
-        def body(i):
+    def feed(self, slot, first, count):
+        def body(n):
+            i = first + n
             t, p = lax.div(i, 2), lax.rem(i, 2)
             at, cols = row_tile(t), lane_tile(p, 512)
             w_up, w_down = self.wup[slot, :, cols], self.wdown[slot, cols, :]
@@ -211,7 +226,7 @@
             self.out[at, :] += nn(g, w_down)
             self.grad[at, :] += nt(du, w_up)
 
-        loop(2 * TILES, body)
+        loop(count, body)
 
     def norm2_back(self):
         def body(t):
@@ -320,20 +335,21 @@
 
         loop(TILES, body)
 
-    def norm1_back(self):
-        def body(t):
+    def norm1_back(self, first, count):
+        def body(n):
+            t = first + n
             at = row_tile(t)
             grad = jnp.zeros((TILE, WIDE), F32)
             for hh in range(2):
                 for c in range(3):
                     part = self.dqkv[c * TILES + t, :, hh * 256 : (hh + 1) * 256]
-                    grad = grad + nt(part, self.wqkv[hh, :, c * 256 : (c + 1) * 256])
+                    grad = grad + nt(part, self.wqkv[hh, c])
             hat, rstd = centre(self.tokens[at, :].astype(F32))
             self.small[0:1, :] += jnp.sum(grad * hat, axis=0, keepdims=True)
             self.small[2:3, :] += jnp.sum(grad, axis=0, keepdims=True)
             self.grad[at, :] += centre_back(grad, hat, rstd, self.gains[0:1, :])
 
-        loop(TILES, body)
+        loop(count, body)
 
 
 def work_buffers():
@@ -356,13 +372,11 @@
         rstd2=vmem((ROWS, 128), F32),
         g=vmem((TILES * 4, 256, 512), BF16),
         du=vmem((TILES * 4, 256, 512), BF16),
-        dhb=vmem((ROWS, WIDE), BF16),
         dnx=vmem((PAIRS, ROWS, 256), BF16),
         zsend=vmem((PAIRS, 144, 256), BF16),
         gsend=vmem((PAIRS, 144, 256), BF16),
         xt=vmem((WIDE, ROWS), BF16),
         xt2=vmem((WIDE, ROWS), BF16),
-        small=vmem((4, WIDE), F32),
     )
 
 
@@ -413,29 +427,45 @@
         )
 
 
-    def weight(self, i):
+    def parts(self, i):
         source = (self.wqkv_in, self.wout_in, self.wup_in, self.wdown_in)[i]
-        return source, (self.wqkv, self.wout, self.wup, self.wdown)[i], source.shape[0] // 2
+        slots = (self.wqkv, self.wout, self.wup, self.wdown)[i]
+        size = source.shape[-2] // (2 if i < 2 else 4)
+
+        def cut(ref, p):
+            here = pl.ds(pl.multiple_of(p * size, size), size)
+            return ref.at[:, here] if i == 0 else ref.at[here]
+
+        return source, slots, cut
+
+    def part(self, i, far=False):
+        if i < 2:
+            return self.core
+        return 2 * ((1 - self.x) if far else self.x) + self.core
 
     def own_weight(self, i):
-        source, slots, _ = self.weight(i)
+        source, slots, _ = self.parts(i)
         return pltpu.make_async_copy(source, slots.at[self.me], self.own_sems.at[i])
 
-    def weight_over(self, i):
-        source, slots, half = self.weight(i)
-        part = pl.ds(pl.multiple_of(self.core * half, half), half)
-        target = slots.at[self.me, part]
-        return self.copy(source.at[part], target, self.over_sems, i, self.place("y"))
-
-    def weight_along(self, i):
-        _, slots, half = self.weight(i)
-        part = pl.ds(pl.multiple_of(self.core * half, half), half)
-        held = slots.at[1 - self.me, part]
-        return self.copy(held, held, self.along_sems, i, self.place("core"))
+    def over(self, i):
+        source, slots, cut = self.parts(i)
+        p = self.part(i)
+        target = cut(slots.at[self.me], p)
+        return self.copy(cut(source, p), target, self.over_sems, i, self.place("y"))
+
+    def across(self, i):
+        _, slots, cut = self.parts(i)
+        held = cut(slots.at[1 - self.me], self.part(i))
+        return self.copy(held, held, self.across_sems, i - 2, self.place("x"))
+
+    def along(self, i, far=False):
+        _, slots, cut = self.parts(i)
+        held = cut(slots.at[1 - self.me], self.part(i, far))
+        return self.copy(held, held, self.along_sems, i + (2 if far else 0), self.place("core"))
 
 
     def axes(self, seg):
-        return ("y", "x") if seg != 1 else ("x", "y")
+        return ("y", "x") if seg % 2 == 0 else ("x", "y")
 
     def index(self, axis):
         return self.me if axis == "y" else self.x
@@ -490,53 +520,47 @@
         for step in range(1, self.deep):
             self.z_copy(seg, step).start()
 
-    def finish_z(self, seg, out):
+    def finish_z(self, seg):
         start, _ = self.mine(seg, 2)
         here = pl.ds(pl.multiple_of(start + self.z * self.block, self.block), self.block)
         total = self.grads[seg][self.core, here].astype(F32)
         for step in range(1, self.deep):
             self.z_copy(seg, step).wait()
             total = total + self.got[seg][3][step - 1].astype(F32)
-        out[...] = total
-
-
-    def small_sum(self, small, heard):
-        slot = 0
-        for axis in ("core", "y", "x"):
-            both = self.copy(small, heard.at[slot], self.small_sems, slot, self.place(axis))
+        return total
+
+
+    def small_copies(self, stage):
+        if stage < 3:
+            places = [self.place(("core", "y", "x")[stage])]
+        else:
+            places = [self.place("z", s) for s in range(1, self.deep)]
+        return [
+            self.copy(self.small.at[stage], self.heard.at[stage + n], self.small_sems, stage + n, where)
+            for n, where in enumerate(places)
+        ]
+
+    def small_start(self, stage):
+        for both in self.small_copies(stage):
             both.start()
+
+    def small_finish(self, stage):
+        total = self.small[stage]
+        for n, both in enumerate(self.small_copies(stage)):
             both.wait()
-            small[...] = small[...] + heard[slot]
-            slot += 1
-        copies = [
-            self.copy(small, heard.at[2 + s], self.small_sems, 2 + s, self.place("z", s))
-            for s in range(1, self.deep)
-        ]
-        for both in copies:
-            both.start()
-        for both in copies:
-            both.wait()
-        total = small[...]
-        for s in range(1, self.deep):
-            total = total + heard[2 + s]
-        return total
-
-
-def scatter(grads, deep, c_of):
+            total = total + self.heard[stage + n]
+        self.small[stage + 1] = total
+
+
+def by_owner(ref, flipped, deep, total, tensor, lanes):
     block = WIDE // (4 * deep)
-
-    def store(c, total):
-        tensor, col = c_of(c)
-        low = total.astype(BF16)
-        for d in range(4 * deep):
-            core, x, z = d % 2, d // 2 % 2, d // 4
-            ref, flipped = grads
-            near, far = (x, tensor) if flipped else (tensor, x)
-            row = ((near * 2 + far) * deep + z) * block
-            here = pl.ds(pl.multiple_of(row, block), block)
-            ref[core, here, lane_tile(col, TILE)] = low[d * block : (d + 1) * block]
-
-    return store
+    low = total.astype(BF16)
+    for d in range(4 * deep):
+        core, x, z = d % 2, d // 2 % 2, d // 4
+        near, far = (x, tensor) if flipped else (tensor, x)
+        row = ((near * 2 + far) * deep + z) * block
+        here = pl.ds(pl.multiple_of(row, block), block)
+        ref[core, here, lanes] = low[d * block : (d + 1) * block]
 
 
 def layer_kernel(deep, names, *refs):
@@ -546,102 +570,118 @@
         deep,
         dict(
             r,
-            grads=(r["grads0"], r["grads1"], r["wup"]),
-            got=tuple(tuple(r[f"got{d}"].at[s] for d in range(4)) for s in range(3)),
-            sum_sems=tuple(sends.at[s] for s in range(3)),
+            grads=tuple(r[f"grads{s}"] for s in range(4)),
+            got=tuple(tuple(r[f"got{s}_{d}"] for d in range(4)) for s in range(4)),
+            sum_sems=tuple(sends.at[s] for s in range(4)),
         ),
     )
-    p = Phases(**r, dqkv=r["du"])
+    p = Phases(**dict(r, dqkv=r["du"], dhb=r["hat2"], small=r["small"].at[0]))
     me = links.me
     other = 1 - me
 
     links.greet()
     for i in range(4):
         links.own_weight(i).start()
+    cot_in = pltpu.make_async_copy(r["cot_in"], p.cot, r["io_sems"].at[0])
+    cot_in.start()
     p.set_up()
     links.met()
     for i in range(2):
-        links.weight_over(i).start()
+        links.over(i).start()
     p.norm1()
     links.own_weight(0).wait()
     p.project(me)
 
-    def pairs_of(ref, hh):
-        return ref.at[pl.ds(2 * hh, 2)]
-
-    def sums_to(source, target, sems, at, hh):
-        return links.copy(pairs_of(source, hh), pairs_of(target, hh), sems, at, links.place("y"))
+    def z_copy(hh):
+        here = pl.ds(2 * hh, 2)
+        return links.copy(p.zsend.at[here], p.zgot.at[here], r["z_sems"], hh, links.place("y"))
 
     @pl.when(me == 0)
     def _():
         p.zgot[...] = jnp.zeros(p.zgot.shape, BF16)
-        sums_to(p.zsend, p.zgot, r["z_sems"], 0, 0).start()
+        z_copy(0).start()
 
     @pl.when(me == 1)
     def _():
         p.ggot[...] = jnp.zeros(p.ggot.shape, BF16)
 
-    for i in range(2):
-        links.weight_over(i).wait()
-        links.weight_along(i).start()
-    links.weight_along(0).wait()
+    links.over(2).start()
+    p.attend_near(me)
+    links.over(0).wait()
+    links.along(0).start()
+    links.along(0).wait()
     p.project(other)
 
     @pl.when(me == 0)
     def _():
-        sums_to(p.zsend, p.zgot, r["z_sems"], 1, 1).start()
-
-    for i in range(2, 4):
-        links.weight_over(i).start()
-
-    @pl.when(me == 1)
-    def _():
-        for hh in range(2):
-            sums_to(p.zsend, p.zgot, r["z_sems"], hh, hh).wait_recv()
-
-    for hh in (me, other):
-        p.attend(hh, lambda j: p.unpack(p.zgot[j]))
-
-    @pl.when(me == 0)
-    def _():
-        for hh in range(2):
-            sums_to(p.zsend, p.zgot, r["z_sems"], hh, hh).wait_send()
+        z_copy(1).start()
+
+    links.over(3).start()
+    links.over(1).wait()
+    links.along(1).start()
+    p.attend_near(other)
+    links.over(2).wait()
+    links.across(2).start()
+    links.along(2).start()
+    for hh in range(2):
+
+        @pl.when(me == 1)
+        def _():
+            z_copy(hh).wait_recv()
+
+        for jj in range(2):
+            p.attend_far(2 * hh + jj, lambda j: p.unpack(p.zgot[j]))
+
+        @pl.when(me == 0)
+        def _():
+            z_copy(hh).wait_send()
 
     links.own_weight(1).wait()
-    links.weight_along(1).wait()
+    links.along(1).wait()
     p.norm2()
     links.own_weight(2).wait()
     links.own_weight(3).wait()
-    p.feed(me)
+    cot_in.wait()
+    p.feed(me, 0, 4)
+    links.across(2).wait()
+    links.along(2, True).start()
+    links.over(3).wait()
+    links.across(3).start()
+    links.along(3).start()
+    p.feed(me, 4, 4)
+    links.across(3).wait()
+    links.along(3, True).start()
     for i in range(2, 4):
-        links.weight_over(i).wait()
-        links.weight_along(i).start()
-    for i in range(2, 4):
-        links.weight_along(i).wait()
-    p.feed(other)
+        links.along(i).wait()
+        links.along(i, True).wait()
+    p.feed(other, 0, 8)
+    out_copy = pltpu.make_async_copy(p.out, r["out_hbm"], r["io_sems"].at[1])
+    out_copy.start()
 
     p.norm2_back()
     p.attend_back_start()
     loop(PAIRS, p.sums_back)
-
-    def grad_sums():
-        return links.copy(p.gsend, p.ggot, r["g_sems"], 0, links.place("y"))
+    g_copy = links.copy(p.gsend, p.ggot, r["g_sems"], 0, links.place("y"))
 
     @pl.when(me == 1)
     def _():
-        grad_sums().start()
-
-    def by_ff(c):
-        return lax.div(c, 4), lax.rem(c, 4)
-
-    def half_block(ref):
-        return lambda t, c: ref[t * 4 + lax.div(c, 2), :, lane_tile(lax.rem(c, 2), TILE)]
+        g_copy.start()
+
+    def ff_grad(xt, blocks, seg):
+        def store(c, total):
+            lanes = lane_tile(lax.rem(c, 4), TILE)
+            by_owner(links.grads[seg], seg == 1, deep, total, lax.div(c, 4), lanes)
+
+        def take(t, c):
+            return blocks[t * 4 + lax.div(c, 2), :, lane_tile(lax.rem(c, 2), TILE)]
+
+        p.weight_grad(xt, take, 8, store)
 
     p.flip(p.n2, p.xt)
-    p.weight_grad(p.xt, half_block(p.du), 8, scatter((links.grads[0], False), deep, by_ff))
+    ff_grad(p.xt, p.du, 0)
     links.start(0, 0)
     p.flip(p.cot, p.xt2)
-    p.weight_grad(p.xt2, half_block(p.g), 8, scatter((links.grads[1], True), deep, by_ff))
+    ff_grad(p.xt2, p.g, 1)
     links.start(1, 0)
     links.finish(0, 0)
     links.start(0, 1)
@@ -650,59 +690,100 @@
         p.xt,
         lambda t, c: p.a[pl.ds(t * TILE, TILE), lane_tile(c, TILE)],
         2,
-        scatter((links.grads[2], False), deep, lambda c: (c, 0)),
+        lambda c, total: by_owner(links.grads[2], False, deep, total, c, slice(0, TILE)),
     )
     links.finish(1, 0)
     links.start(1, 1)
-    return p, links, r
-
-
-def layer_rest(deep, p, links, r):
-    me = links.me
-    loop(2, p.back_q)
-    loop(2, lambda j: p.back_q(j + 2))
+    p.flip(p.n1, p.xt2)
+    loop(PAIRS, p.back_q)
     for seg in range(2):
         links.finish(seg, 1)
         links.start(seg, 2)
 
-    def grad_sums():
-        return links.copy(p.gsend, p.ggot, r["g_sems"], 0, links.place("y"))
-
     @pl.when(me == 0)
     def _():
-        grad_sums().wait_recv()
+        g_copy.wait_recv()
 
     @pl.when(me == 1)
     def _():
-        grad_sums().wait_send()
+        g_copy.wait_send()
 
     def back(j):
         p.back_kv(j, lambda j: p.unpack(p.ggot[j]))
 
-    loop(2, back)
+    def qkv_grad(seg):
+        pieces = [(hh, c) for hh in range(2) for c in range(3)]
+        base = (0, 0, TILE, 0)[seg]
+        for n in range(3):
+            total = jnp.zeros((WIDE, TILE), F32)
+            for t in range(TILES):
+                rows = [
+                    p.dqkv[c * TILES + t, :, lane_tile(2 * hh + seg - 2)]
+                    for hh, c in pieces[2 * n : 2 * n + 2]
+                ]
+                total = total + nn(
+                    p.xt2[:, t * TILE : (t + 1) * TILE], jnp.concatenate(rows, axis=1)
+                )
+            for half, (hh, c) in enumerate(pieces[2 * n : 2 * n + 2]):
+                by_owner(
+                    links.grads[seg],
+                    seg == 3,
+                    deep,
+                    total[:, half * 128 : (half + 1) * 128],
+                    hh,
+                    pl.ds(base + c * 128, 128),
+                )
+
+    back(0)
+    back(2)
     for seg in range(2):
         links.finish(seg, 2)
         links.start_z(seg)
-    loop(2, lambda j: back(j + 2))
-    p.flip(p.n1, p.xt2)
-    p.weight_grad(
-        p.xt2,
-        lambda t, c: p.dqkv[lax.div(c, 2) * TILES + t, :, lane_tile(lax.rem(c, 2), TILE)],
-        6,
-        scatter((links.grads[2], False), deep, lambda c: (lax.rem(c, 2), 1 + lax.div(c, 2))),
-    )
+    qkv_grad(2)
     links.start(2, 0)
-    p.norm1_back()
+    back(1)
     links.finish(2, 0)
     links.start(2, 1)
-    for seg in range(2):
-        links.finish_z(seg, p.owned.at[seg])
-    p.norms[...] = links.small_sum(p.small, p.heard)
+    back(3)
+    qkv_grad(3)
+    links.start(3, 0)
+    r["own_up"][...] = links.finish_z(0)
+    r["own_down"][...] = links.finish_z(1)
+    p.norm1_back(0, 2)
+    links.finish(3, 0)
+    links.start(3, 1)
+    p.norm1_back(2, 2)
+    grad_copy = pltpu.make_async_copy(p.grad, r["grad_hbm"], r["io_sems"].at[2])
+    grad_copy.start()
+    links.small_start(0)
     links.finish(2, 1)
     links.start(2, 2)
+    links.small_finish(0)
+    links.small_start(1)
+    links.finish(3, 1)
+    links.start(3, 2)
+    links.small_finish(1)
+    links.small_start(2)
     links.finish(2, 2)
     links.start_z(2)
-    links.finish_z(2, p.owned.at[2])
+    links.finish(3, 2)
+    links.start_z(3)
+    links.small_finish(2)
+    links.small_start(3)
+
+    def own_qkv(total, jj):
+        for c in range(3):
+            r["own_qkv"][c, :, jj * 128 : (jj + 1) * 128] = total[:, c * 128 : (c + 1) * 128]
+
+    total = links.finish_z(2)
+    r["own_wout"][...] = total[:, :TILE]
+    own_qkv(total[:, TILE:], 0)
+    own_qkv(links.finish_z(3), 1)
+    links.small_finish(3)
+    r["own_gains"][...] = r["small"][4, 0:2]
+    r["own_shifts"][...] = r["small"][4, 2:4]
+    out_copy.wait()
+    grad_copy.wait()
 
 
 def layer_call(deep, tokens, cotangent, wqkv, wout, wup, wdown, gains, shifts, fresh, last, flags):
@@ -710,7 +791,7 @@
     block = WIDE // (4 * deep)
     inputs = dict(
         tokens=(tokens, vmem),
-        cot=(cotangent, vmem),
+        cot_in=(cotangent, hbm),
         wqkv_in=(wqkv, hbm),
         wout_in=(wout, hbm),
         wup_in=(wup, hbm),
@@ -722,45 +803,55 @@
         flags=(flags, pltpu.SMEM),
     )
     outputs = dict(
-        out=jax.ShapeDtypeStruct((ROWS, WIDE), F32),
-        grad=jax.ShapeDtypeStruct((ROWS, WIDE), F32),
-        owned=jax.ShapeDtypeStruct((3, block, OWNED), F32),
-        norms=jax.ShapeDtypeStruct((4, WIDE), F32),
+        out_hbm=((ROWS, WIDE), hbm),
+        grad_hbm=((ROWS, WIDE), hbm),
+        own_qkv=((3, block, 256), vmem),
+        own_wout=((block, 256), vmem),
+        own_up=((block, 1024), vmem),
+        own_down=((block, 1024), vmem),
+        own_gains=((2, WIDE), vmem),
+        own_shifts=((2, WIDE), vmem),
     )
     dma = pltpu.SemaphoreType.DMA
+    widths = (1024, 1024, 640, 384)
     scratch = dict(
         work_buffers(),
-        wqkv=vmem((2, WIDE, 768), BF16),
+        out=vmem((ROWS, WIDE), F32),
+        grad=vmem((ROWS, WIDE), F32),
+        cot=vmem((ROWS, WIDE), BF16),
+        wqkv=vmem((2, 3, WIDE, 256), BF16),
         wout=vmem((2, 256, WIDE), BF16),
         wup=vmem((2, WIDE, 1024), BF16),
         wdown=vmem((2, 1024, WIDE), BF16),
         zgot=vmem((PAIRS, 144, 256), BF16),
         ggot=vmem((PAIRS, 144, 256), BF16),
-        grads0=vmem((2, WIDE, OWNED), BF16),
-        grads1=vmem((2, WIDE, OWNED), BF16),
-        got0=vmem((3, WIDE, OWNED), BF16),
-        got1=vmem((3, WIDE // 2, OWNED), BF16),
-        got2=vmem((3, WIDE // 4, OWNED), BF16),
-        got3=vmem((3, deep - 1, block, OWNED), BF16),
+        small=vmem((5, 4, WIDE), F32),
         heard=vmem((2 + deep, 4, WIDE), F32),
         own_sems=dma((4,)),
         over_sems=dma((8,)),
-        along_sems=dma((8,)),
+        across_sems=dma((4,)),
+        along_sems=dma((12,)),
         z_sems=dma((4,)),
         g_sems=dma((2,)),
-        sum_sems=dma((3, 2 * (2 + deep))),
+        io_sems=dma((3,)),
+        sum_sems=dma((4, 2 * (2 + deep))),
         small_sems=dma((2 * (2 + deep),)),
     )
+    for seg, width in enumerate(widths):
+        scratch[f"grads{seg}"] = vmem((2, WIDE, width), BF16)
+        for depth in range(3):
+            scratch[f"got{seg}_{depth}"] = vmem((WIDE // 2**depth, width), BF16)
+        scratch[f"got{seg}_3"] = vmem((deep - 1, block, width), BF16)
     names = (*inputs, *outputs, *scratch)
 
     def kernel(*refs):
-        layer_rest(deep, *layer_kernel(deep, names, *refs))
+        layer_kernel(deep, names, *refs)
 
     return pl.pallas_call(
         kernel,
-        out_shape=tuple(outputs.values()),
+        out_shape=tuple(jax.ShapeDtypeStruct(shape, F32) for shape, _ in outputs.values()),
         in_specs=[pl.BlockSpec(memory_space=space) for _, space in inputs.values()],
-        out_specs=tuple(pl.BlockSpec(memory_space=vmem) for _ in outputs),
+        out_specs=tuple(pl.BlockSpec(memory_space=space) for _, space in outputs.values()),
         scratch_shapes=list(scratch.values()),
         compiler_params=pltpu.CompilerParams(
             collective_id=0, has_side_effects=True, vmem_limit_bytes=67043328
@@ -773,11 +864,12 @@
     tokens, cotangent, w_qkv, w_out, w_up, w_down, gains, shifts, feat_fresh, feat_last, flags
 ):
     deep = lax.axis_size("dp") // 4
-    result, grad_tokens, owned, norms = layer_call(
+    by_part = jnp.transpose(w_qkv, (1, 0, 2))
+    outs = layer_call(
         deep,
         tokens,
         cotangent,
-        w_qkv.reshape(WIDE, 768),
+        by_part,
         w_out,
         w_up,
         w_down,
@@ -787,16 +879,16 @@
         feat_last,
         flags,
     )
-    rest = owned[2]
+    result, grad_tokens, own_qkv, own_wout, own_up, own_down, own_gains, own_shifts = outs
     return (
         result,
         grad_tokens,
-        rest[:, 256:].reshape(-1, 3, 256),
-        rest[:, :256].T,
-        owned[0],
-        owned[1].T,
-        norms[:2],
-        norms[2:],
+        jnp.transpose(own_qkv, (1, 0, 2)),
+        own_wout.T,
+        own_up,
+        own_down.T,
+        own_gains,
+        own_shifts,
     )
 
 

time: 159 us -> 135 us (0.85)
  Pallas kernels: 146 us -> 126 us
  local copies, waits for them, and re-layouts: 11.5 us -> 8.33 us
    pallas_call x1, Pallas kernels: 146 us -> 126 us  [layer_call(): pl.pallas_call(kernel, out_shape=tuple((jax.ShapeDtypeStruct(shape, F32)...]
    transpose x2 -> x0, local copies, waits for them, and re-layouts: 2.37 us -> none  [the longest x1 1.75 us: fused(): owned[1]]
    unnamed x5 -> x22, local copies, waits for them, and re-layouts: 5.96 us -> 8.33 us
    reshape x2 -> x0, local copies, waits for them, and re-layouts: 1.8 us -> none  [the longest x1 1.15 us: fused(): w_qkv.reshape(WIDE, 768)]
where the time goes in v3:
time: 135 us
  Pallas kernels  126 us (93%)
  local copies, waits for them, and re-layouts  8.33 us (6%)
    pallas_call x1, Pallas kernels, layer_call(): pl.pallas_call(kernel, out_shape=tuple((jax.ShapeDtypeStruct(shape, F32)...  126 us
    unnamed x22, local copies, waits for them, and re-layouts  8.33 us

profile of v3, /device:TPU:0, one launch (start us, length us, event | category | flops | bytes accessed | tf_op | source)
XLA Modules:
  0.0 134.5 jit_solution(18044036634569739349)
XLA Ops:
  0.6 125.5 %layer.1 = (f32[1024,512]{1,0:T(8,128)}, f32[1024,512]{1,0:T(8,128)}, f32[3,32,256]{2,1,0:T(8,128)}, f32[32,256]{1,0:T(8,128)}, f32[32,1024]{1,0:T(8,128)}, /*in...) custom-call(bf16[1024,512]{1,0:T(8,128)(2,1)} %refs_0_.1, bf16[1024,512]{1,0:T(8,128)(2,1)} %refs_1_.1, ...), custom_call_target="tpu_custom_call" | custom-call | tf_op jit(solution)/shard_map/layer/pallas_call | solution.py:850
  126.2 0.0 copy-start
  126.2 3.2 %copy.27 = f32[1024,512]{1,0:T(8,128)} copy(f32[1024,512]{1,0:T(8,128)} %get-tuple-element.32) | data formatting | bytes 4194304
  129.4 0.0 copy-done
  129.4 0.0 copy-start.3
  129.4 0.0 copy-start.4
  129.4 0.0 copy-start.2
  129.4 0.0 copy-start.1
  129.4 0.0 copy-start.6
  129.4 0.0 copy-start.5
  129.4 1.3 copy.28
  130.8 0.0 copy-done.3
  130.8 0.6 copy.29
  131.4 0.0 copy-done.4
  131.4 0.6 copy.30
  132.0 0.0 copy-done.2
  132.0 0.7 copy.31
  132.7 0.0 copy-done.1
  132.7 0.7 copy.32
  133.3 0.0 copy-done.6
  133.3 0.6 copy.33
  133.9 0.0 copy-done.5
  133.9 0.6 copy.34
Async XLA Ops:
  126.2 3.2 %copy-start = (f32[1024,512]{1,0:T(8,128)S(1)}, f32[1024,512]{1,0:T(8,128)}, u32[]{:S(2)}) copy-start(f32[1024,512]{1,0:T(8,128)} %get-tuple-element.33) | copy-start | bytes 6291460
  129.4 1.4 %copy-start.3 = (f32[3,32,256]{2,1,0:T(8,128)S(1)}, f32[3,32,256]{2,1,0:T(8,128)}, u32[]{:S(2)}) copy-start(f32[3,32,256]{2,1,0:T(8,128)} %get-tuple-element.18) | copy-start | bytes 294916
  129.4 2.0 %copy-start.4 = (f32[32,256]{1,0:T(8,128)S(1)}, f32[32,256]{1,0:T(8,128)}, u32[]{:S(2)}) copy-start(f32[32,256]{1,0:T(8,128)} %get-tuple-element.19) | copy-start | bytes 98308
  129.4 2.6 %copy-start.2 = (f32[32,1024]{1,0:T(8,128)S(1)}, f32[32,1024]{1,0:T(8,128)}, u32[]{:S(2)}) copy-start(f32[32,1024]{1,0:T(8,128)} %get-tuple-element.36) | copy-start | bytes 393220
  129.4 3.3 %copy-start.1 = (f32[32,1024]{1,0:T(8,128)S(1)}, f32[32,1024]{1,0:T(8,128)}, u32[]{:S(2)}) copy-start(f32[32,1024]{1,0:T(8,128)} %get-tuple-element.21) | copy-start | bytes 393220
  129.4 3.9 %copy-start.6 = (f32[2,512]{1,0:T(2,128)S(1)}, f32[2,512]{1,0:T(2,128)}, u32[]{:S(2)}) copy-start(f32[2,512]{1,0:T(2,128)} %get-tuple-element.38) | copy-start | bytes 12292
  129.4 4.5 %copy-start.5 = (f32[2,512]{1,0:T(2,128)S(1)}, f32[2,512]{1,0:T(2,128)}, u32[]{:S(2)}) copy-start(f32[2,512]{1,0:T(2,128)} %get-tuple-element.39) | copy-start | bytes 12292

commit v4 on v3

--- a/solution.py
+++ b/solution.py
@@ -32,8 +32,8 @@
     return lax.broadcasted_iota(jnp.int32, shape, dim)
 
 
-def row_tile(t):
-    return pl.ds(pl.multiple_of(t * TILE, TILE), TILE)
+def row_tile(t, size=TILE):
+    return pl.ds(pl.multiple_of(t * size, size), size)
 
 
 def lane_tile(j, width=128):
@@ -85,6 +85,10 @@
     return FACTOR * through[:, :half] + (FACTOR * FACTOR) * through[:, half:] * rows.astype(F32)
 
 
+def with_ones(values):
+    return jnp.concatenate([values, jnp.ones_like(values)], axis=1)
+
+
 def merge_heads(state):
     own = of_head((state.shape[0], FEATURES), 0, 0)
     return jnp.where(own, state[:, :FEATURES], state[:, FEATURES:])
@@ -95,7 +99,6 @@
         self.__dict__.update(refs)
 
     def set_up(self):
-        self.vx[:, :, 128:] = jnp.ones((PAIRS, ROWS, 128), BF16)
         fresh, last = self.fresh[...], self.last[...]
         zero = jnp.zeros((HEAD_DIM, FEATURES), BF16)
         minus = jnp.full((HEAD_DIM, FEATURES), -1.0, BF16)
@@ -112,10 +115,11 @@
 
     def norm1(self):
         def body(t):
-            hat, _ = centre(self.tokens[row_tile(t), :].astype(F32))
-            self.n1[row_tile(t), :] = (hat * self.gains[0:1, :] + self.shifts[0:1, :]).astype(BF16)
-
-        loop(TILES, body)
+            at = row_tile(t, 128)
+            hat, _ = centre(self.tokens[at, :].astype(F32))
+            self.n1[at, :] = (hat * self.gains[0:1, :] + self.shifts[0:1, :]).astype(BF16)
+
+        loop(ROWS // 128, body)
 
     def project(self, hh):
         for jj in range(2):
@@ -131,12 +135,12 @@
                 q, k, v = (p[:, jj * 128 : (jj + 1) * 128] for p in parts)
                 self.q[j, row_tile(t), :] = q
                 self.k[j, row_tile(t), :] = k
-                self.vx[j, row_tile(t), 0:128] = v
+                self.vx[j, row_tile(t), :] = v
                 wf = self.wf[j]
                 self.phi_q[j, row_tile(t), :] = features_of(q, wf)
                 phi_k = features_of(k, wf)
                 self.phi_k[j, row_tile(t), :] = phi_k
-                state = merge_heads(tn(self.vx[j, row_tile(t), :], phi_k))
+                state = merge_heads(tn(with_ones(v), phi_k))
                 self.zt[j * TILES + t] = state.astype(BF16)
                 self.run[jj] += state
 
@@ -159,12 +163,10 @@
         return jnp.concatenate([low[0:128], *sums], axis=0)
 
     def attend_near(self, hh):
-        for jj in range(2):
-            j = 2 * hh + jj
-
-            def body(t, j=j):
-                at = row_tile(t)
-                vx = self.vx[j, at, :]
+        def body(t):
+            at = row_tile(t)
+            for j in (2 * hh, 2 * hh + 1):
+                vx = with_ones(self.vx[j, at, :])
                 both = []
                 for head in range(2):
                     f = slice(head * FEATURES, (head + 1) * FEATURES)
@@ -175,26 +177,29 @@
                 self.out[at, lane_tile(j)] = r[:, :128]
                 self.grad[at, lane_tile(j)] = r[:, 128:]
 
-            loop(TILES, body)
-
-    def attend_far(self, j, start):
-        self.run[0] = start(j)
+        loop(TILES, body)
+
+    def attend_far(self, hh, start):
+        for jj in range(2):
+            self.run[jj] = start(2 * hh + jj)
 
         def body(t):
             at = row_tile(t)
-            before = self.run[0]
-            low = before.astype(BF16)
-            self.run[0] = before + self.zt[j * TILES + t].astype(F32)
-            self.zt[j * TILES + t] = low
-            both = [
-                nt(self.phi_q[j, at, head * FEATURES : (head + 1) * FEATURES], low)
-                for head in range(2)
-            ]
-            r = jnp.where(of_head(both[0].shape, 1, 0), both[0], both[1])
-            inverse = 1.0 / (r[:, 128:] + self.grad[at, lane_tile(j)])
-            num = r[:, :128] + self.out[at, lane_tile(j)]
-            self.a[at, lane_tile(j)] = (num * inverse).astype(BF16)
-            self.inverse[j, at, :] = inverse
+            for jj in range(2):
+                j = 2 * hh + jj
+                before = self.run[jj]
+                low = before.astype(BF16)
+                self.run[jj] = before + self.zt[j * TILES + t].astype(F32)
+                self.zt[j * TILES + t] = low
+                both = [
+                    nt(self.phi_q[j, at, head * FEATURES : (head + 1) * FEATURES], low)
+                    for head in range(2)
+                ]
+                r = jnp.where(of_head(both[0].shape, 1, 0), both[0], both[1])
+                inverse = 1.0 / (r[:, 128:] + self.grad[at, lane_tile(j)])
+                num = r[:, :128] + self.out[at, lane_tile(j)]
+                self.a[at, lane_tile(j)] = (num * inverse).astype(BF16)
+                self.inverse[j, at, :] = inverse
 
         loop(TILES, body)
 
@@ -212,25 +217,42 @@
 
         loop(TILES, body)
 
-    def feed(self, slot, first, count):
+    def feed_in(self, step, me):
+        at, cols, slot, place = self.feed_place(step, me)
+        g, slope = gelu_and_slope(nn(self.n2[at, :], self.wup[slot, :, cols]))
+        self.g[place] = g.astype(BF16)
+        self.du[place] = (slope * nt(self.cot[at, :], self.wdown[slot, cols, :])).astype(BF16)
+
+    def feed_back(self, step, me):
+        at, cols, slot, place = self.feed_place(step, me)
+        self.grad[at, :] += nt(self.du[place], self.wup[slot, :, cols])
+
+    def feed_place(self, step, me):
+        late = lax.div(step, 2 * TILES)
+        slot = me + late * (1 - 2 * me)
+        t, p = lax.div(lax.rem(step, 2 * TILES), 2), lax.rem(step, 2)
+        return row_tile(t), lane_tile(p, 512), slot, t * 4 + slot * 2 + p
+
+    def feed(self, first, count, me):
         def body(n):
-            i = first + n
-            t, p = lax.div(i, 2), lax.rem(i, 2)
-            at, cols = row_tile(t), lane_tile(p, 512)
-            w_up, w_down = self.wup[slot, :, cols], self.wdown[slot, cols, :]
-            g, slope = gelu_and_slope(nn(self.n2[at, :], w_up))
-            g = g.astype(BF16)
-            du = (slope * nt(self.cot[at, :], w_down)).astype(BF16)
-            self.g[t * 4 + slot * 2 + p] = g
-            self.du[t * 4 + slot * 2 + p] = du
-            self.out[at, :] += nn(g, w_down)
-            self.grad[at, :] += nt(du, w_up)
+            self.feed_back(first + n - 1, me)
+            self.feed_in(first + n, me)
 
         loop(count, body)
+
+    def feed_out(self):
+        def body(t):
+            total = self.out[row_tile(t), :]
+            for n in range(4):
+                w_down = self.wdown[n // 2, (n % 2) * 512 : (n % 2) * 512 + 512, :]
+                total = total + nn(self.g[t * 4 + n], w_down)
+            self.out[row_tile(t), :] = total
+
+        loop(TILES, body)
 
     def norm2_back(self):
         def body(t):
-            at = row_tile(t)
+            at = row_tile(t, 128)
             grad, hat = self.grad[at, :], self.hat2[at, :].astype(F32)
             self.small[1:2, :] += jnp.sum(grad * hat, axis=0, keepdims=True)
             self.small[3:4, :] += jnp.sum(grad, axis=0, keepdims=True)
@@ -239,7 +261,7 @@
             self.grad[at, :] = dh
             self.dhb[at, :] = dh.astype(BF16)
 
-        loop(TILES, body)
+        loop(ROWS // 128, body)
 
     def flip(self, source, out):
         def body(t):
@@ -248,13 +270,14 @@
         loop(TILES, body)
 
     def weight_grad(self, xt, blocks, n_cols, store):
-        def body(c):
-            total = nn(xt[:, 0:TILE], blocks(0, c))
-            for t in range(1, TILES):
-                total = total + nn(xt[:, t * TILE : (t + 1) * TILE], blocks(t, c))
-            store(c, total)
-
-        loop(n_cols, body)
+        def body(i):
+            for c in (2 * i, 2 * i + 1):
+                total = nn(xt[:, 0:TILE], blocks(0, c))
+                for t in range(1, TILES):
+                    total = total + nn(xt[:, t * TILE : (t + 1) * TILE], blocks(t, c))
+                store(c, total)
+
+        loop(n_cols // 2, body)
 
     def attend_back_start(self):
         def body(t):
@@ -277,33 +300,32 @@
         loop(TILES, body)
 
     def sums_back(self, j):
-        self.run[0] = jnp.zeros((TILE, FEATURES), F32)
-
-        def body(t):
-            at = row_tile(t)
+        total = jnp.zeros((TILE, FEATURES), F32)
+        for t in range(TILES):
+            at = slice(t * TILE, (t + 1) * TILE)
             state = merge_heads(tn(self.dnx[j, at, :], self.phi_q[j, at, :]))
             self.gt[j * TILES + t] = state.astype(BF16)
-            self.run[0] += state
-
-        loop(TILES, body)
+            total = total + state
+        self.run[0] = total
         self.pack(self.gsend, j, self.run.at[0], True)
 
     def back_q(self, j):
-        def body(t):
-            at = row_tile(t)
-            dnx = self.dnx[j, at, :]
-            w = []
-            for head in range(2):
-                f = slice(head * FEATURES, (head + 1) * FEATURES)
-                own = jnp.where(of_head(dnx.shape, 1, head), dnx, jnp.zeros_like(dnx))
-                ds = nt(own, self.vx[j, at, :])
-                ds = jnp.where(iota(ds.shape, 1) <= iota(ds.shape, 0), ds, 0.0).astype(BF16)
-                dphi = nn(ds, self.phi_k[j, at, f]) + nn(own, self.zt[j * TILES + t])
-                w.append((dphi * self.phi_q[j, at, f].astype(F32)).astype(BF16))
-            dq = features_back(self.q[j, at, :], self.wf[j], jnp.concatenate(w, axis=1))
-            self.dqkv[0 * TILES + t, :, lane_tile(j)] = dq.astype(BF16)
-
-        loop(TILES, body)
+        def body(i):
+            for t in (2 * i, 2 * i + 1):
+                at = row_tile(t)
+                dnx = self.dnx[j, at, :]
+                w = []
+                for head in range(2):
+                    f = slice(head * FEATURES, (head + 1) * FEATURES)
+                    own = jnp.where(of_head(dnx.shape, 1, head), dnx, jnp.zeros_like(dnx))
+                    ds = nt(own, with_ones(self.vx[j, at, :]))
+                    ds = jnp.where(iota(ds.shape, 1) <= iota(ds.shape, 0), ds, 0.0).astype(BF16)
+                    dphi = nn(ds, self.phi_k[j, at, f]) + nn(own, self.zt[j * TILES + t])
+                    w.append((dphi * self.phi_q[j, at, f].astype(F32)).astype(BF16))
+                dq = features_back(self.q[j, at, :], self.wf[j], jnp.concatenate(w, axis=1))
+                self.dqkv[0 * TILES + t, :, lane_tile(j)] = dq.astype(BF16)
+
+        loop(TILES // 2, body)
 
     def back_kv(self, j, start):
         self.run[0] = start(j)
@@ -314,7 +336,7 @@
             after = self.run[0]
             low = after.astype(BF16)
             self.run[0] = after + self.gt[j * TILES + t].astype(F32)
-            dnx, vx = self.dnx[j, at, :], self.vx[j, at, :]
+            dnx, vx = self.dnx[j, at, :], with_ones(self.vx[j, at, :])
             w, dv = [], []
             for head in range(2):
                 f = slice(head * FEATURES, (head + 1) * FEATURES)
@@ -358,7 +380,7 @@
         n1=vmem((ROWS, WIDE), BF16),
         q=vmem((PAIRS, ROWS, 128), BF16),
         k=vmem((PAIRS, ROWS, 128), BF16),
-        vx=vmem((PAIRS, ROWS, 256), BF16),
+        vx=vmem((PAIRS, ROWS, 128), BF16),
         phi_q=vmem((PAIRS, ROWS, 512), BF16),
         phi_k=vmem((PAIRS, ROWS, 512), BF16),
         zt=vmem((PAIRS * TILES, 256, 256), BF16),
@@ -428,39 +450,41 @@
 
 
     def parts(self, i):
-        source = (self.wqkv_in, self.wout_in, self.wup_in, self.wdown_in)[i]
-        slots = (self.wqkv, self.wout, self.wup, self.wdown)[i]
-        size = source.shape[-2] // (2 if i < 2 else 4)
+        if i < 3:
+            source, slots = self.wqkv_in.at[i], [self.wqkv.at[t, i] for t in (self.me, 1 - self.me)]
+        else:
+            source = (self.wout_in, self.wup_in, self.wdown_in)[i - 3]
+            whole = (self.wout, self.wup, self.wdown)[i - 3]
+            slots = [whole.at[t] for t in (self.me, 1 - self.me)]
+        size = source.shape[-2] // (2 if i < 4 else 4)
 
         def cut(ref, p):
-            here = pl.ds(pl.multiple_of(p * size, size), size)
-            return ref.at[:, here] if i == 0 else ref.at[here]
-
-        return source, slots, cut
+            return ref.at[pl.ds(pl.multiple_of(p * size, size), size)]
+
+        return source, *slots, cut
 
     def part(self, i, far=False):
-        if i < 2:
+        if i < 4:
             return self.core
         return 2 * ((1 - self.x) if far else self.x) + self.core
 
     def own_weight(self, i):
-        source, slots, _ = self.parts(i)
-        return pltpu.make_async_copy(source, slots.at[self.me], self.own_sems.at[i])
+        source, mine, _, _ = self.parts(i)
+        return pltpu.make_async_copy(source, mine, self.own_sems.at[i])
 
     def over(self, i):
-        source, slots, cut = self.parts(i)
+        source, mine, _, cut = self.parts(i)
         p = self.part(i)
-        target = cut(slots.at[self.me], p)
-        return self.copy(cut(source, p), target, self.over_sems, i, self.place("y"))
+        return self.copy(cut(source, p), cut(mine, p), self.over_sems, i, self.place("y"))
 
     def across(self, i):
-        _, slots, cut = self.parts(i)
-        held = cut(slots.at[1 - self.me], self.part(i))
-        return self.copy(held, held, self.across_sems, i - 2, self.place("x"))
+        _, _, other, cut = self.parts(i)
+        held = cut(other, self.part(i))
+        return self.copy(held, held, self.across_sems, i - 4, self.place("x"))
 
     def along(self, i, far=False):
-        _, slots, cut = self.parts(i)
-        held = cut(slots.at[1 - self.me], self.part(i, far))
+        _, _, other, cut = self.parts(i)
+        held = cut(other, self.part(i, far))
         return self.copy(held, held, self.along_sems, i + (2 if far else 0), self.place("core"))
 
 
@@ -580,16 +604,17 @@
     other = 1 - me
 
     links.greet()
-    for i in range(4):
+    for i in range(6):
         links.own_weight(i).start()
     cot_in = pltpu.make_async_copy(r["cot_in"], p.cot, r["io_sems"].at[0])
     cot_in.start()
     p.set_up()
     links.met()
-    for i in range(2):
+    for i in range(4):
         links.over(i).start()
     p.norm1()
-    links.own_weight(0).wait()
+    for i in range(3):
+        links.own_weight(i).wait()
     p.project(me)
 
     def z_copy(hh):
@@ -605,58 +630,59 @@
     def _():
         p.ggot[...] = jnp.zeros(p.ggot.shape, BF16)
 
-    links.over(2).start()
+    links.over(4).start()
     p.attend_near(me)
-    links.over(0).wait()
-    links.along(0).start()
-    links.along(0).wait()
+    for i in range(3):
+        links.over(i).wait()
+        links.along(i).start()
+    for i in range(3):
+        links.along(i).wait()
     p.project(other)
 
     @pl.when(me == 0)
     def _():
         z_copy(1).start()
 
-    links.over(3).start()
-    links.over(1).wait()
-    links.along(1).start()
+    links.over(5).start()
+    links.over(3).wait()
+    links.along(3).start()
     p.attend_near(other)
-    links.over(2).wait()
-    links.across(2).start()
-    links.along(2).start()
+    links.over(4).wait()
+    links.across(4).start()
+    links.along(4).start()
     for hh in range(2):
 
         @pl.when(me == 1)
         def _():
             z_copy(hh).wait_recv()
 
-        for jj in range(2):
-            p.attend_far(2 * hh + jj, lambda j: p.unpack(p.zgot[j]))
+        p.attend_far(hh, lambda j: p.unpack(p.zgot[j]))
 
         @pl.when(me == 0)
         def _():
             z_copy(hh).wait_send()
 
-    links.own_weight(1).wait()
-    links.along(1).wait()
+    links.own_weight(3).wait()
+    links.along(3).wait()
     p.norm2()
-    links.own_weight(2).wait()
-    links.own_weight(3).wait()
+    links.own_weight(4).wait()
+    links.own_weight(5).wait()
     cot_in.wait()
-    p.feed(me, 0, 4)
-    links.across(2).wait()
-    links.along(2, True).start()
-    links.over(3).wait()
-    links.across(3).start()
-    links.along(3).start()
-    p.feed(me, 4, 4)
-    links.across(3).wait()
-    links.along(3, True).start()
-    for i in range(2, 4):
+    p.feed_in(0, me)
+    p.feed(1, 3, me)
+    links.across(4).wait()
+    links.along(4, True).start()
+    links.over(5).wait()
+    links.across(5).start()
+    links.along(5).start()
+    p.feed(4, 4, me)
+    links.across(5).wait()
+    links.along(5, True).start()
+    for i in range(4, 6):
         links.along(i).wait()
         links.along(i, True).wait()
-    p.feed(other, 0, 8)
-    out_copy = pltpu.make_async_copy(p.out, r["out_hbm"], r["io_sems"].at[1])
-    out_copy.start()
+    p.feed(8, 8, me)
+    p.feed_back(15, me)
 
     p.norm2_back()
     p.attend_back_start()
@@ -683,8 +709,6 @@
     p.flip(p.cot, p.xt2)
     ff_grad(p.xt2, p.g, 1)
     links.start(1, 0)
-    links.finish(0, 0)
-    links.start(0, 1)
     p.flip(p.dhb, p.xt)
     p.weight_grad(
         p.xt,
@@ -692,13 +716,13 @@
         2,
         lambda c, total: by_owner(links.grads[2], False, deep, total, c, slice(0, TILE)),
     )
+    p.flip(p.n1, p.xt2)
+    links.finish(0, 0)
+    links.start(0, 1)
+    loop(2, p.back_q)
     links.finish(1, 0)
     links.start(1, 1)
-    p.flip(p.n1, p.xt2)
-    loop(PAIRS, p.back_q)
-    for seg in range(2):
-        links.finish(seg, 1)
-        links.start(seg, 2)
+    loop(2, lambda j: p.back_q(j + 2))
 
     @pl.when(me == 0)
     def _():
@@ -735,20 +759,21 @@
                 )
 
     back(0)
+    for seg in range(2):
+        links.finish(seg, 1)
+        links.start(seg, 2)
     back(2)
-    for seg in range(2):
-        links.finish(seg, 2)
-        links.start_z(seg)
     qkv_grad(2)
     links.start(2, 0)
     back(1)
     links.finish(2, 0)
     links.start(2, 1)
+    for seg in range(2):
+        links.finish(seg, 2)
+        links.start_z(seg)
     back(3)
     qkv_grad(3)
     links.start(3, 0)
-    r["own_up"][...] = links.finish_z(0)
-    r["own_down"][...] = links.finish_z(1)
     p.norm1_back(0, 2)
     links.finish(3, 0)
     links.start(3, 1)
@@ -758,6 +783,11 @@
     links.small_start(0)
     links.finish(2, 1)
     links.start(2, 2)
+    p.feed_out()
+    out_copy = pltpu.make_async_copy(p.out, r["out_hbm"], r["io_sems"].at[1])
+    out_copy.start()
+    r["own_up"][...] = links.finish_z(0)
+    r["own_down"][...] = links.finish_z(1)
     links.small_finish(0)
     links.small_start(1)
     links.finish(3, 1)
@@ -827,10 +857,10 @@
         ggot=vmem((PAIRS, 144, 256), BF16),
         small=vmem((5, 4, WIDE), F32),
         heard=vmem((2 + deep, 4, WIDE), F32),
-        own_sems=dma((4,)),
-        over_sems=dma((8,)),
+        own_sems=dma((6,)),
+        over_sems=dma((12,)),
         across_sems=dma((4,)),
-        along_sems=dma((12,)),
+        along_sems=dma((16,)),
         z_sems=dma((4,)),
         g_sems=dma((2,)),
         io_sems=dma((3,)),
@@ -860,12 +890,48 @@
     )(*(array for array, _ in inputs.values()))
 
 
+def hand_over(arrays):
+    count = len(arrays)
+
+    def kernel(*refs):
+        ins, outs, held = refs[:count], refs[count : 2 * count], refs[2 * count : 3 * count]
+        sems = refs[3 * count]
+        pieces = []
+        for i, array in enumerate(arrays):
+            cuts = 4 if array.shape[0] == ROWS else 1
+            size = array.shape[0] // cuts
+            for n in range(cuts):
+                here = pl.ds(n * size, size)
+                at = len(pieces)
+                fetch = pltpu.make_async_copy(ins[i].at[here], held[i].at[here], sems.at[0, at])
+                store = pltpu.make_async_copy(held[i].at[here], outs[i].at[here], sems.at[1, at])
+                pieces.append((fetch, store))
+        for fetch, _ in pieces:
+            fetch.start()
+        for fetch, store in pieces:
+            fetch.wait()
+            store.start()
+        for _, store in pieces:
+            store.wait()
+
+    anywhere = pl.BlockSpec(memory_space=pl.ANY)
+    return pl.pallas_call(
+        kernel,
+        out_shape=tuple(jax.ShapeDtypeStruct(a.shape, a.dtype) for a in arrays),
+        in_specs=[anywhere] * count,
+        out_specs=(anywhere,) * count,
+        scratch_shapes=[pltpu.VMEM(a.shape, a.dtype) for a in arrays]
+        + [pltpu.SemaphoreType.DMA((2, 16))],
+        name="hand_over",
+    )(*arrays)
+
+
 def fused(
     tokens, cotangent, w_qkv, w_out, w_up, w_down, gains, shifts, feat_fresh, feat_last, flags
 ):
     deep = lax.axis_size("dp") // 4
     by_part = jnp.transpose(w_qkv, (1, 0, 2))
-    outs = layer_call(
+    outs = hand_over(layer_call(
         deep,
         tokens,
         cotangent,
@@ -878,7 +944,7 @@
         feat_fresh,
         feat_last,
         flags,
-    )
+    ))
     result, grad_tokens, own_qkv, own_wout, own_up, own_down, own_gains, own_shifts = outs
     return (
         result,

time: 135 us -> 123 us (0.911)
  local copies, waits for them, and re-layouts: 8.33 us -> 0 us
  Pallas kernels: 126 us -> 122 us
    unnamed x22 -> x0, local copies, waits for them, and re-layouts: 8.33 us -> none
    pallas_call x1, Pallas kernels: 126 us -> 118 us  [layer_call(): pl.pallas_call(kernel, out_shape=tuple((jax.ShapeDtypeStruct(shape, F32)...]
    pallas_call x0 -> x1, Pallas kernels: none -> 3.99 us  [hand_over(): pl.pallas_call(kernel, out_shape=tuple((jax.ShapeDtypeStruct(a.shape, a.d...]
where the time goes in v4:
time: 123 us
  Pallas kernels  122 us (99%)
    pallas_call x1, Pallas kernels, layer_call(): pl.pallas_call(kernel, out_shape=tuple((jax.ShapeDtypeStruct(shape, F32)...  118 us
    pallas_call x1, Pallas kernels, hand_over(): pl.pallas_call(kernel, out_shape=tuple((jax.ShapeDtypeStruct(a.shape, a.d...  3.99 us

profile of v4, /device:TPU:0, one launch (start us, length us, event | category | flops | bytes accessed | tf_op | source)
XLA Modules:
  0.0 122.6 jit_solution(15390700824076324518)
XLA Ops:
  0.6 117.8 %layer.1 = (f32[1024,512]{1,0:T(8,128)}, f32[1024,512]{1,0:T(8,128)}, f32[3,32,256]{2,1,0:T(8,128)}, f32[32,256]{1,0:T(8,128)}, f32[32,1024]{1,0:T(8,128)}, /*in...) custom-call(bf16[1024,512]{1,0:T(8,128)(2,1)} %refs_0_.1, bf16[1024,512]{1,0:T(8,128)(2,1)} %refs_1_.1, ...), custom_call_target="tpu_custom_call" | custom-call | tf_op jit(solution)/shard_map/layer/pallas_call | solution.py:880
  118.4 4.0 %hand_over.1 = (f32[1024,512]{1,0:T(8,128)}, f32[1024,512]{1,0:T(8,128)}, f32[3,32,256]{2,1,0:T(8,128)}, f32[32,256]{1,0:T(8,128)}, f32[32,1024]{1,0:T(8,128)}, ...) custom-call(f32[1024,512]{1,0:T(8,128)} %get-tuple-element.24.refs_0_, ...), custom_call_target="tpu_custom_call" | custom-call | tf_op jit(solution)/shard_map/hand_over/pallas_call | solution.py:918
